TPU v7x, 16 devices: a whole 2x2x2 slice. The times are simulated.
16 devices in a mesh: rep: 1, dp: 16 (over x, y, z, core).
Axes of the slice: x: 2, y: 2, z: 2, core: 2. Of those that a mesh axis runs over, the one named last changes fastest.
Arguments:
- g_w_gate: bfloat16 [16, 2, 1024, 3072], P(('rep', 'dp'))
- g_w_up: bfloat16 [16, 2, 1024, 3072], P(('rep', 'dp'))
- g_w_down: bfloat16 [16, 2, 3072, 1024], P(('rep', 'dp'))
- w_gate: bfloat16 [2, 1024, 3072], replicated
- w_up: bfloat16 [2, 1024, 3072], replicated
- w_down: bfloat16 [2, 3072, 1024], replicated
- m_w_gate: float32 [2, 1024, 3072], P(None, 'dp')
- m_w_up: float32 [2, 1024, 3072], P(None, 'dp')
- m_w_down: float32 [2, 3072, 1024], P(None, 'dp')
- v_w_gate: float32 [2, 1024, 3072], P(None, 'dp')
- v_w_up: float32 [2, 1024, 3072], P(None, 'dp')
- v_w_down: float32 [2, 3072, 1024], P(None, 'dp')
Outputs:
- output 1: bfloat16 [2, 1024, 3072], P('rep')
- output 2: bfloat16 [2, 1024, 3072], P('rep')
- output 3: bfloat16 [2, 3072, 1024], P('rep')
- output 4: float32 [2, 1024, 3072], P('rep', 'dp')
- output 5: float32 [2, 1024, 3072], P('rep', 'dp')
- output 6: float32 [2, 3072, 1024], P('rep', 'dp')
- output 7: float32 [2, 1024, 3072], P('rep', 'dp')
- output 8: float32 [2, 1024, 3072], P('rep', 'dp')
- output 9: float32 [2, 3072, 1024], P('rep', 'dp')
All inputs are finite; a program needn't handle non-finite values.
Results may differ from a plain program's by a relative error of at most 0.022.
Values are sent between devices in bfloat16 or wider.
A program may use at most 2 GiB of HBM per device.

v0:
```python
import functools

import jax
import jax.numpy as jnp
from jax import lax
from jax.experimental import pallas as pl
from jax.experimental.pallas import tpu as pltpu
from jax.sharding import PartitionSpec as P


X, Y, Z = 4, 2, 1
ORDERS = ((X, Y, Z), (Y, Z, X), (Z, X, Y))
LAYERS = 2
HALVES = 2
CHUNKS = tuple((layer, half) for layer in range(LAYERS) for half in range(HALVES))
LAST = len(CHUNKS) - 1
TILE = 16
VMEM = 15 * 512 * 1024
THEIRS, LAND1, LAND2, LAND3, OLD = 0, 8, 12, 14, 15
RING = 12
STAGES = ((0, 4), (4, 2), (6, 1), (7, 1))


def ring():
    order = [(stage, c) for stage in range(4) for c in range(len(CHUNKS))]
    place, then, holder, unit = {}, {}, {}, 0
    for stage, c in order:
        count = STAGES[stage][1]
        place[stage, c] = unit % RING
        blocks = [(unit + i) % RING for i in range(count)]
        before = [holder[b] for b in blocks if b in holder]
        then.setdefault(max(before, key=order.index) if before else None, []).append((stage, c))
        holder.update({b: (stage, c) for b in blocks})
        unit += count
    return place, then


PLACE, THEN = ring()
TURN = {0: (0, 1, 1, 0), 1: (1, 1, 1, 1), 2: (0, 0, 0, 0), 3: (1, 1, 1, 1)}
FIRST = {(0, 0): 4, (0, 1): 8, (0, 3): 4, (1, 0): 8, (2, 0): 4, (3, 0): 4}


def slots(order):
    d1, d2, d3 = order
    kept = [d2 ^ d3, d2, d3, 0]
    return [d1 ^ r for r in kept] + kept


def total(refs):
    acc = refs[0].astype(jnp.float32)
    for one in refs[1:]:
        acc = acc + one.astype(jnp.float32)
    return acc


def kernel(*refs):
    g, w, m, v, out_w, out_m, out_v, later, mine = (refs[i : i + 3] for i in range(0, 27, 3))
    (pair_send, pair_first, pair_recv, pair_kept, mine_sem, rs_send, rs_recv) = refs[27:34]
    (state_sem, free, ag_send, agp_send) = refs[34:]

    me = lax.axis_index("dp")
    core = lax.rem(me, 2)
    bits = {Z: lax.rem(lax.div(me, 2), 2), Y: lax.rem(lax.div(me, 4), 2), X: lax.div(me, 8)}

    def chip(mask):
        return sum(d * ((1 - bits[d]) if mask & d else bits[d]) for d in (X, Y, Z))

    def at(mask):
        return {"dp": chip(mask) * 2 + core}

    partner = {"dp": me + 1 - 2 * core}
    peers = (partner, at(X), at(Y), at(Z))
    rows_of = [one.shape[1] for one in m]

    def rows(k, mask, which, half):
        size = rows_of[k] // HALVES
        start = (chip(mask) * 2 + which) * rows_of[k] + half * size
        return pl.ds(pl.multiple_of(start, TILE), size)

    def part(k, half, slot=0):
        size = rows_of[k] // HALVES
        return pl.ds(slot * rows_of[k] + half * size, size)

    def remote(src, dst, send, recv, device):
        return pltpu.make_async_remote_copy(
            src_ref=src, dst_ref=dst, send_sem=send, recv_sem=recv, device_id=device, device_id_type=pl.DeviceIdType.MESH
        )

    events = [(c, layer, half, k) for c, (layer, half) in enumerate(CHUNKS) for k in range(3)]

    def load_mine(k, after):
        for stage, c in THEN.get(after, []):
            layer, half = CHUNKS[c]
            first, count = STAGES[stage]
            for j, r in enumerate(slots(ORDERS[k])[first : first + count]):
                source = g[k].at[layer, rows(k, r, core, half)]
                pltpu.make_async_copy(source, mine[k].at[PLACE[stage, c] + j], mine_sem.at[TURN[stage][c], k]).start()

    def pair(k, c, layer, half, slot):
        r = slots(ORDERS[k])[slot]
        arrived = pair_kept.at[k] if slot > 3 else pair_recv.at[k, c - 1] if c else pair_first.at[k, slot]
        here = out_w[k].at[layer, part(k, half, THEIRS + slot)]
        return remote(g[k].at[layer, rows(k, r, 1 - core, half)], here, pair_send.at[k], arrived, partner)

    for k in range(3):
        load_mine(k, None)

    barrier = pltpu.get_barrier_semaphore()
    for peer in peers:
        pl.semaphore_signal(barrier, inc=1, device_id=peer, device_id_type=pl.DeviceIdType.MESH)
    pl.semaphore_wait(barrier, 4)

    def pair_chunk(c, group):
        for slot in range(4 * group, 4 * group + 4):
            for k in range(3):
                pair(k, c, *CHUNKS[c], slot).start()

    pair_chunk(0, 0)
    pair_chunk(1, 0)

    def arrival(k, blocks, sem):
        spot = out_w[k].at[0, pl.ds(0, blocks * rows_of[k] // HALVES)]
        return remote(spot, spot, pair_send.at[k], sem, partner)

    def departure(k, blocks, sem):
        spot = out_w[k].at[0, pl.ds(0, blocks * rows_of[k] // HALVES)]
        return remote(spot, spot, sem, pair_kept.at[k], partner)

    def wait_mine(k, c, stage):
        if (stage, c) in FIRST:
            spot = mine[k].at[pl.ds(0, FIRST[stage, c])]
            pltpu.make_async_copy(spot, spot, mine_sem.at[TURN[stage][c], k]).wait()

    def step_of(k):
        return TILE * (1 if k < 2 else 3)

    def slot_rows(k, half, slot, i):
        return pl.ds(pl.multiple_of(slot * rows_of[k] + half * (rows_of[k] // HALVES) + i * step_of(k), TILE), step_of(k))

    def add(k, c, layer, half, stage, begin, count, extra):
        first = STAGES[stage][0] + begin
        steps = rows_of[k] // HALVES // step_of(k)

        def body(n, _):
            j, i = lax.div(n, steps), lax.rem(n, steps)
            here = slot_rows(k, half, THEIRS + first + j, i)
            terms = [out_w[k][layer, here], mine[k][PLACE[stage, c] + begin + j, slot_rows(k, 0, 0, i)]]
            terms += [out_w[k][layer, slot_rows(k, half, slot + j, i)] for slot in extra]
            out_w[k][layer, here] = total(terms).astype(jnp.bfloat16)
            return 0

        lax.fori_loop(0, count * steps, body, 0)

    def hop(stage, k, c, layer, half, begin, count):
        first = STAGES[stage][0]
        land = (LAND1, LAND2, LAND3)[stage]
        for j in range(begin, begin + count):
            source = out_w[k].at[layer, part(k, half, THEIRS + first + j)]
            target = out_w[k].at[layer, part(k, half, land + j)]
            remote(source, target, rs_send.at[k, c], rs_recv.at[stage, k, c], at(ORDERS[k][stage])).start()

    for slot in range(4):
        for k in range(3):
            if slot == 0:
                wait_mine(k, 0, 0)
            arrival(k, 1, pair_first.at[k, slot]).wait_recv()
            add(k, 0, *CHUNKS[0], 0, slot, 1, [])
            hop(0, k, 0, *CHUNKS[0], slot, 1)
    for c, group in ((2, 0), (3, 0), (0, 1), (1, 1), (2, 1), (3, 1)):
        pair_chunk(c, group)
    for k in range(3):
        load_mine(k, (0, 0))
    for c, layer, half, k in events[3:]:
        wait_mine(k, c, 0)
        arrival(k, 4, pair_recv.at[k, c - 1]).wait_recv()
        add(k, c, layer, half, 0, 0, 4, [])
        hop(0, k, c, layer, half, 0, 4)
        load_mine(k, (0, c))

    def state(k, layer, half):
        here = part(k, half)
        return [
            pltpu.make_async_copy(w[k].at[layer, rows(k, 0, core, half)], out_w[k].at[layer, part(k, half, OLD)], state_sem.at[k]),
            pltpu.make_async_copy(m[k].at[layer, here], out_m[k].at[layer, here], state_sem.at[k]),
            pltpu.make_async_copy(v[k].at[layer, here], out_v[k].at[layer, here], state_sem.at[k]),
        ]

    for c, layer, half, k in events:
        for copy in state(k, layer, half):
            copy.start()

    for c, layer, half, k in events:
        if c == 0:
            arrival(k, 4 * len(CHUNKS), pair_kept.at[k]).wait_recv()
        wait_mine(k, c, 1)
        arrival(k, 4, rs_recv.at[0, k, c]).wait_recv()
        add(k, c, layer, half, 1, 0, 2, [LAND1])
        hop(1, k, c, layer, half, 0, 2)
        load_mine(k, (1, c))
    for c, layer, half, k in events:
        wait_mine(k, c, 2)
        arrival(k, 2, rs_recv.at[1, k, c]).wait_recv()
        add(k, c, layer, half, 2, 0, 1, [LAND1 + 2, LAND2])
        hop(2, k, c, layer, half, 0, 1)

    def adamw(k, c, layer, half):
        steps = rows_of[k] // HALVES // step_of(k)

        def body(i, _):
            here = slot_rows(k, half, 0, i)
            terms = [out_w[k][layer, slot_rows(k, half, slot, i)] for slot in (THEIRS + 7, LAND1 + 3, LAND2 + 1, LAND3)]
            terms.append(mine[k][PLACE[3, c], slot_rows(k, 0, 0, i)])
            grad = total(terms).astype(jnp.bfloat16).astype(jnp.float32)
            old = out_w[k][layer, slot_rows(k, half, OLD, i)].astype(jnp.float32)
            new_m = 0.9 * out_m[k][layer, here] + 0.1 * grad
            new_v = 0.95 * out_v[k][layer, here] + 0.05 * grad * grad
            out_m[k][layer, here] = new_m
            out_v[k][layer, here] = new_v
            new = old - 0.02 * (new_m * lax.rsqrt(new_v + 1e-8) + 0.1 * old)
            out_w[k][layer, slot_rows(k, half, me, i)] = new.astype(jnp.bfloat16)
            return 0

        lax.fori_loop(0, steps, body, 0)

    def gathered(k, c, mask):
        d1, d2, d3 = ORDERS[k]
        if not mask & d1:
            return rs_recv.at[(d3, d2, d2 ^ d3).index(mask), k, c]
        return pair_first.at[k, (0, d3, d2, d2 ^ d3).index(mask ^ d1)] if c == LAST - 1 else pair_recv.at[k, c]

    def set_aside(k, layer, half, mask, place):
        start = (chip(mask) * 2 + core) * rows_of[k] + half * (rows_of[k] // HALVES)

        def body(i, _):
            there = pl.ds(pl.multiple_of(start + i * step_of(k), TILE), step_of(k))
            later[k][place, slot_rows(k, 0, 0, i)] = out_w[k][layer, there]
            return 0

        lax.fori_loop(0, rows_of[k] // HALVES // step_of(k), body, 0)

    def gather(k, c, layer, half, mask, dim):
        _, d2, d3 = ORDERS[k]
        d = ORDERS[k][dim]
        spot = out_w[k].at[layer, rows(k, mask, core, half)]
        if dim == 0 and c == LAST:
            set_aside(k, layer, half, mask, (0, d3, d2, d2 ^ d3).index(mask))
        else:
            remote(spot, spot, ag_send.at[k], gathered(k, c, mask ^ d), at(d)).start()

    def wait_gather(k, c, mask):
        arrival(k, 1, gathered(k, c, mask)).wait_recv()

    def to_partner(k, layer, half, mask):
        spot = out_w[k].at[layer, rows(k, mask, core, half)]
        return remote(spot, spot, agp_send.at[k], pair_kept.at[k], partner)

    def send_own(c, layer, half, k):
        pl.semaphore_wait(free.at[k, c], 4)
        for dim in (2, 1, 0):
            gather(k, c, layer, half, 0, dim)
        to_partner(k, layer, half, 0).start()

    for n, (c, layer, half, k) in enumerate(events):
        if c == 0:
            held = out_w[k].at[0, pl.ds(0, 10 * rows_of[k])]
            pltpu.make_async_copy(held, held, state_sem.at[k]).wait()
        wait_mine(k, c, 3)
        arrival(k, 1, rs_recv.at[2, k, c]).wait_recv()
        departure(k, 7, rs_send.at[k, c]).wait_send()
        adamw(k, c, layer, half)
        for peer in peers:
            pl.semaphore_signal(free.at[k, c], inc=1, device_id=peer, device_id_type=pl.DeviceIdType.MESH)
        if n:
            send_own(*events[n - 1])
    send_own(*events[-1])

    for c, layer, half, k in events:
        d1, d2, d3 = ORDERS[k]
        wait_gather(k, c, d3)
        for dim in (1, 0):
            gather(k, c, layer, half, d3, dim)
        to_partner(k, layer, half, d3).start()
    for c, (layer, half) in enumerate(CHUNKS):
        for far in range(2):
            for k, (d1, d2, d3) in enumerate(ORDERS):
                mask = d2 ^ d3 * far
                wait_gather(k, c, mask)
                gather(k, c, layer, half, mask, 0)
                to_partner(k, layer, half, mask).start()
    for c, (layer, half) in enumerate(CHUNKS[:LAST]):
        for which in range(4):
            for k, (d1, d2, d3) in enumerate(ORDERS):
                if c == LAST - 1:
                    arrival(k, 1, pair_first.at[k, which]).wait_recv()
                elif which == 0:
                    arrival(k, 4, pair_recv.at[k, c]).wait_recv()
                to_partner(k, layer, half, d1 ^ (0, d3, d2, d2 ^ d3)[which]).start()

    n = len(CHUNKS)
    for k in range(3):
        departure(k, 8 * n, pair_send.at[k]).wait_send()
        departure(k, 7 * n - 4, ag_send.at[k]).wait_send()
        departure(k, 8 * n - 4, agp_send.at[k]).wait_send()
        arrival(k, 8 * n - 4, pair_kept.at[k]).wait_recv()


def put_out(*refs):
    sources, targets, sem = refs[:9], refs[9:18], refs[18]
    for i, (source, target) in enumerate(zip(sources, targets, strict=True)):
        for layer in range(LAYERS):
            for j in range(4):
                here = pl.ds(j * (source.shape[1] // 4), source.shape[1] // 4)
                pltpu.make_async_copy(source.at[layer, here], target.at[layer, here], sem.at[i]).start()
    for i, (source, target) in enumerate(zip(sources, targets, strict=True)):
        pltpu.make_async_copy(source, target, sem.at[i]).wait()


def put_rest(items, *refs):
    n = len(items)
    sources, out_w, sem = refs[:n], refs[n + 3 : n + 6], refs[n + 6]
    me = lax.axis_index("dp")
    core = lax.rem(me, 2)
    bits = {Z: lax.rem(lax.div(me, 2), 2), Y: lax.rem(lax.div(me, 4), 2), X: lax.div(me, 8)}
    layer, half = CHUNKS[LAST]
    for i, (k, whose) in enumerate(items):
        d1, d2, d3 = ORDERS[k]
        size = sources[i].shape[1]
        for j, r in enumerate((0, d3, d2, d2 ^ d3)):
            chip = sum(d * ((1 - bits[d]) if (d1 ^ r) & d else bits[d]) for d in (X, Y, Z))
            which = 1 - core if whose else core
            start = ((chip * 2 + which) * HALVES + half) * size
            target = out_w[k].at[layer, pl.ds(pl.multiple_of(start, TILE), size)]
            pltpu.make_async_copy(sources[i].at[j], target, sem.at[i]).start()
    for i in range(n):
        pltpu.make_async_copy(sources[i], sources[i], sem.at[i]).wait()


def solution(mesh):
    def step(*arrays):
        terms = [one.reshape(one.shape[1:]) for one in arrays[:3]]
        weights, m, v = arrays[3:6], arrays[6:9], arrays[9:12]
        blocks = [one.shape[1:] for one in m]
        n = len(CHUNKS)

        dma = pltpu.SemaphoreType.DMA
        out = pl.pallas_call(
            kernel,
            out_shape=[pltpu.VMEM(one.shape, one.dtype) for one in (*weights, *m, *v)]
            + [pltpu.VMEM((4, rows // HALVES, columns), jnp.bfloat16) for rows, columns in blocks],
            in_specs=[pl.BlockSpec(memory_space=pl.ANY)] * 12,
            out_specs=[pl.BlockSpec(memory_space=pltpu.VMEM)] * 12,
            scratch_shapes=[
                *[pltpu.VMEM((RING, rows // HALVES, columns), jnp.bfloat16) for rows, columns in blocks],
                dma((3,)),
                dma((3, 4)),
                dma((3, n - 1)),
                dma((3,)),
                dma((2, 3)),
                dma((3, n)),
                dma((3, 3, n)),
                dma((3,)),
                pltpu.SemaphoreType.REGULAR((3, n)),
                dma((3,)),
                dma((3,)),
            ],
            compiler_params=pltpu.CompilerParams(collective_id=0, has_side_effects=True, vmem_limit_bytes=VMEM),
            name="step",
        )(*terms, *weights, *m, *v)
        out, later = out[:9], out[9:]
        own = []
        for k in range(3):
            own.append(lax.ppermute(later[k], "dp", [(i, i ^ 2 * ORDERS[k][0]) for i in range(16)]))
        out = pl.pallas_call(
            put_out,
            out_shape=[jax.ShapeDtypeStruct(one.shape, one.dtype) for one in (*weights, *m, *v)],
            in_specs=[pl.BlockSpec(memory_space=pl.ANY)] * 9,
            out_specs=[pl.BlockSpec(memory_space=pl.ANY)] * 9,
            scratch_shapes=[dma((9,))],
            cost_estimate=pl.CostEstimate(flops=30_000_000, bytes_accessed=48_000_000, transcendentals=0),
            compiler_params=pltpu.CompilerParams(vmem_limit_bytes=VMEM),
            name="put_out",
        )(*out)
        swap = [(i, i ^ 1) for i in range(16)]
        own[0], out = lax.optimization_barrier((own[0], out))
        other = [lax.ppermute(own[0], "dp", swap)]
        own, out, other = lax.optimization_barrier((own, out, other))
        other += [lax.ppermute(one, "dp", swap) for one in own[1:]]
        arrived = {(k, whose): (own, other)[whose][k] for k in range(3) for whose in range(2)}
        new = out[:3]
        for items in (((0, 0), (1, 0), (2, 0), (0, 1)), ((1, 1), (2, 1))):
            n = len(items)
            new = pl.pallas_call(
                functools.partial(put_rest, items),
                out_shape=[jax.ShapeDtypeStruct(one.shape, one.dtype) for one in weights],
                in_specs=[pl.BlockSpec(memory_space=pltpu.VMEM)] * n + [pl.BlockSpec(memory_space=pl.ANY)] * 3,
                out_specs=[pl.BlockSpec(memory_space=pl.ANY)] * 3,
                scratch_shapes=[dma((n,))],
                input_output_aliases={n: 0, n + 1: 1, n + 2: 2},
                cost_estimate=pl.CostEstimate(flops=3_000_000, bytes_accessed=5_000_000, transcendentals=0),
                compiler_params=pltpu.CompilerParams(vmem_limit_bytes=VMEM),
                name="put_rest",
            )(*[arrived[item] for item in items], *new)
        out = [*new, *out[3:]]
        return tuple(out)

    all_of, cut = P(None, None, None), P(None, "dp", None)
    step = jax.shard_map(
        step,
        mesh=mesh,
        in_specs=(P(("rep", "dp"), None, None, None),) * 3 + (all_of,) * 3 + (cut,) * 6,
        out_specs=(P("rep", None, None),) * 3 + (P("rep", "dp", None),) * 6,
        check_vma=False,
    )
    return step
```

profile of v0, /device:TPU:0, one launch (start us, length us, event | category | flops | bytes accessed | tf_op | source)
XLA Modules:
  0.0 256.0 jit_solution(1182913295349923845)
XLA Ops:
  0.6 228.9 %step.1 = (bf16[2,1024,3072]{2,1,0:T(8,128)(2,1)S(1)}, bf16[2,1024,3072]{2,1,0:T(8,128)(2,1)S(1)}, bf16[2,3072,1024]{2,1,0:T(8,128)(2,1)S(1)}, f32[2,64,3072]{2,...) custom-call(bf16[2,1024,3072]{2,1,0:T(8,128)(2,1)} %bitcast.3, ...), custom_call_target="tpu_custom_call" | custom-call | tf_op jit(solution)/shard_map/step/pallas_call | solution.py:346
  229.5 1.5 collective-permute-start
  231.0 0.8 collective-permute-start.1
  231.8 1.2 collective-permute-start.2
  233.1 15.0 %put_out.1 = (bf16[2,1024,3072]{2,1,0:T(8,128)(2,1)}, bf16[2,1024,3072]{2,1,0:T(8,128)(2,1)}, bf16[2,3072,1024]{2,1,0:T(8,128)(2,1)}, f32[2,64,3072]{2,1,0:T(8,1...) custom-call(bf16[2,1024,3072]{2,1,0:T(8,128)(2,1)S(1)} %get-tuple-el, ...), custom_call_target="tpu_custom_call" | custom-call | flops 30000000 | bytes 48000000 | tf_op jit(solution)/shard_map/put_out/pallas_call | solution.py:373
  248.1 1.1 collective-permute-done.refs_0_
  249.1 0.0 collective-permute-start.3
  249.1 1.2 collective-permute-done.1.refs_1_
  250.3 0.8 collective-permute-done.2.refs_2_
  251.1 0.3 collective-permute-done.3.refs_3_
  251.4 0.1 collective-permute-start.4
  251.6 0.4 collective-permute-start.5
  251.9 1.7 put_rest.2
  253.6 0.1 collective-permute-done.4.refs_0_
  253.7 1.1 collective-permute-done.5.refs_1_
  254.8 1.1 put_rest.3
Async XLA Ops:
  229.5 19.6 %collective-permute-start = (bf16[4,32,3072]{2,1,0:T(8,128)(2,1)S(1)}, bf16[4,32,3072]{2,1,0:T(8,128)(2,1)S(1)}, u32[]{:S(2)}, u32[]{:S(2)}) collective-permute-start(bf16[4,32,3072]{2,1,0:T(8,128)(2,1)S(1)} %get-tuple-element.59), channel_id=1, source_target_pairs={{0,8},{1,9},{2,10},{3,11},{4,12},{5,13},{6,14},{7,15},{8,0},{9,1},... | collective-permute-start | bytes 2359304 | tf_op jit(solution)/shard_map/ppermute | solution.py:372
  231.0 19.3 %collective-permute-start.1 = (bf16[4,32,3072]{2,1,0:T(8,128)(2,1)S(1)}, bf16[4,32,3072]{2,1,0:T(8,128)(2,1)S(1)}, u32[]{:S(2)}, u32[]{:S(2)}) collective-permute-start(bf16[4,32,3072]{2,1,0:T(8,128)(2,1)S(1)} %get-tuple-element.79), channel_id=1, source_target_pairs={{0,4},{1,5},{2,6},{3,7},{4,0},{5,1},{6,2},{7,3},{8,12},{9,13},{10,... | collective-permute-start | bytes 2359304 | tf_op jit(solution)/shard_map/ppermute | solution.py:372
  231.8 19.3 %collective-permute-start.2 = (bf16[4,96,1024]{2,1,0:T(8,128)(2,1)S(1)}, bf16[4,96,1024]{2,1,0:T(8,128)(2,1)S(1)}, u32[]{:S(2)}, u32[]{:S(2)}) collective-permute-start(bf16[4,96,1024]{2,1,0:T(8,128)(2,1)S(1)} %get-tuple-element.80), channel_id=1, source_target_pairs={{0,2},{1,3},{2,0},{3,1},{4,6},{5,7},{6,4},{7,5},{8,10},{9,11},{10,... | collective-permute-start | bytes 2359304 | tf_op jit(solution)/shard_map/ppermute | solution.py:372
  249.1 2.3 collective-permute-start.3
  251.4 2.3 collective-permute-start.4
  251.6 3.3 %collective-permute-start.5 = (bf16[4,96,1024]{2,1,0:T(8,128)(2,1)S(1)}, bf16[4,96,1024]{2,1,0:T(8,128)(2,1)S(1)}, u32[]{:S(2)}, u32[]{:S(2)}) collective-permute-start(bf16[4,96,1024]{2,1,0:T(8,128)(2,1)S(1)} %collective-permute-done.2.refs_2_), channel_id=1, source_target_pairs={{0,1},{1,0},{2,3},{3,2},{4,5},{5,4},{6,7},{7,6},{8,9},{9,8},{10,11... | collective-permute-start | bytes 2359304 | tf_op jit(solution)/shard_map/ppermute | solution.py:387
where the time goes:
time: 256 us
  Pallas kernels  247 us (96%)
  waiting for transfers between devices  4.56 us (2%)
  starting transfers between devices  4.06 us (2%)
    pallas_call x1, Pallas kernels, step(): pl.pallas_call(kernel, out_shape=[pltpu.VMEM(one.shape, one.dtype) for on...  229 us
    pallas_call x1, Pallas kernels, step(): pl.pallas_call(put_out, out_shape=[jax.ShapeDtypeStruct(one.shape, one.dt...  15 us
  transfers between devices with their start and end apart: 6, of which 6 were waited for; matrix products, arithmetic and copies ran while one was open for 0% of the time, Pallas kernels for 7%

commit v1 on v0

--- a/solution.py
+++ b/solution.py
@@ -380,11 +380,9 @@
             compiler_params=pltpu.CompilerParams(vmem_limit_bytes=VMEM),
             name="put_out",
         )(*out)
-        swap = [(i, i ^ 1) for i in range(16)]
-        own[0], out = lax.optimization_barrier((own[0], out))
-        other = [lax.ppermute(own[0], "dp", swap)]
-        own, out, other = lax.optimization_barrier((own, out, other))
-        other += [lax.ppermute(one, "dp", swap) for one in own[1:]]
+        other = []
+        for k in range(3):
+            other.append(lax.ppermute(own[k], "dp", [(i, i ^ 1) for i in range(16)]))
         arrived = {(k, whose): (own, other)[whose][k] for k in range(3) for whose in range(2)}
         new = out[:3]
         for items in (((0, 0), (1, 0), (2, 0), (0, 1)), ((1, 1), (2, 1))):

time: 256 us -> 269 us (1.051)
  waiting for transfers between devices: 4.56 us -> 18 us
    ppermute x3, waiting for transfers between devices: 3.03 us -> 18 us  [step(): lax.ppermute(later[k], 'dp', [(i, i ^ 2 * ORDERS[k][0]) for i in range(16)])]
  transfers between devices with their start and end apart: 6 -> 6, of which waited for: 6 -> 3; matrix products, arithmetic and copies ran while one was open for 0% -> 0% of each run, Pallas kernels for 7% -> 6%
where the time goes in v1:
time: 269 us
  Pallas kernels  247 us (92%)
  waiting for transfers between devices  18 us (7%)
  starting transfers between devices  3.55 us (1%)
    pallas_call x1, Pallas kernels, step(): pl.pallas_call(kernel, out_shape=[pltpu.VMEM(one.shape, one.dtype) for on...  229 us
    ppermute x3, waiting for transfers between devices, step(): lax.ppermute(later[k], 'dp', [(i, i ^ 2 * ORDERS[k][0]) for i in range(16)])  18 us
    pallas_call x1, Pallas kernels, step(): pl.pallas_call(put_out, out_shape=[jax.ShapeDtypeStruct(one.shape, one.dt...  15 us
  transfers between devices with their start and end apart: 6, of which 3 were waited for; matrix products, arithmetic and copies ran while one was open for 0% of the time, Pallas kernels for 6%

profile of v1, /device:TPU:0, one launch (start us, length us, event | category | flops | bytes accessed | tf_op | source)
XLA Modules:
  0.0 269.0 jit_solution(16110132506258508375)
XLA Ops:
  0.6 228.9 %step.1 = (bf16[2,1024,3072]{2,1,0:T(8,128)(2,1)S(1)}, bf16[2,1024,3072]{2,1,0:T(8,128)(2,1)S(1)}, bf16[2,3072,1024]{2,1,0:T(8,128)(2,1)S(1)}, f32[2,64,3072]{2,...) custom-call(bf16[2,1024,3072]{2,1,0:T(8,128)(2,1)} %bitcast.3, ...), custom_call_target="tpu_custom_call" | custom-call | tf_op jit(solution)/shard_map/step/pallas_call | solution.py:346
  229.5 1.5 collective-permute-start.4
  231.0 0.8 collective-permute-start
  231.8 1.2 collective-permute-start.2
  233.1 16.1 %collective-permute-done.4.refs_0_ = bf16[4,32,3072]{2,1,0:T(8,128)(2,1)S(1)} collective-permute-done((bf16[4,32,3072]{2,1,0:T(8,128)(2,1)S(1)}, bf16[4,32,3072]{2,1,0:T(8,128)(2,1)S(1)}, u32[]{:S(2)}, u32[]{:S(2)}) %collective-permute-start.4) | collective-permute-done | bytes 786464 | tf_op jit(solution)/shard_map/ppermute | solution.py:372
  249.1 0.0 collective-permute-start.5
  249.1 1.2 collective-permute-done.refs_1_
  250.3 0.0 collective-permute-start.1
  250.3 0.8 collective-permute-done.2.refs_2_
  251.1 0.0 collective-permute-start.3
  251.1 15.0 %put_out.1 = (bf16[2,1024,3072]{2,1,0:T(8,128)(2,1)}, bf16[2,1024,3072]{2,1,0:T(8,128)(2,1)}, bf16[2,3072,1024]{2,1,0:T(8,128)(2,1)}, f32[2,64,3072]{2,1,0:T(8,1...) custom-call(bf16[2,1024,3072]{2,1,0:T(8,128)(2,1)S(1)} %get-tuple-el, ...), custom_call_target="tpu_custom_call" | custom-call | flops 30000000 | bytes 48000000 | tf_op jit(solution)/shard_map/put_out/pallas_call | solution.py:373
  266.1 0.0 collective-permute-done.5.refs_3_
  266.1 1.7 put_rest.2
  267.8 0.0 collective-permute-done.1.refs_0_
  267.9 0.0 collective-permute-done.3.refs_1_
  267.9 1.2 put_rest.3
Async XLA Ops:
  229.5 19.6 %collective-permute-start.4 = (bf16[4,32,3072]{2,1,0:T(8,128)(2,1)S(1)}, bf16[4,32,3072]{2,1,0:T(8,128)(2,1)S(1)}, u32[]{:S(2)}, u32[]{:S(2)}) collective-permute-start(bf16[4,32,3072]{2,1,0:T(8,128)(2,1)S(1)} %get-tuple-element.38), channel_id=1, source_target_pairs={{0,8},{1,9},{2,10},{3,11},{4,12},{5,13},{6,14},{7,15},{8,0},{9,1},... | collective-permute-start | bytes 2359304 | tf_op jit(solution)/shard_map/ppermute | solution.py:372
  231.0 19.3 %collective-permute-start = (bf16[4,32,3072]{2,1,0:T(8,128)(2,1)S(1)}, bf16[4,32,3072]{2,1,0:T(8,128)(2,1)S(1)}, u32[]{:S(2)}, u32[]{:S(2)}) collective-permute-start(bf16[4,32,3072]{2,1,0:T(8,128)(2,1)S(1)} %get-tuple-element.36), channel_id=1, source_target_pairs={{0,4},{1,5},{2,6},{3,7},{4,0},{5,1},{6,2},{7,3},{8,12},{9,13},{10,... | collective-permute-start | bytes 2359304 | tf_op jit(solution)/shard_map/ppermute | solution.py:372
  231.8 19.3 %collective-permute-start.2 = (bf16[4,96,1024]{2,1,0:T(8,128)(2,1)S(1)}, bf16[4,96,1024]{2,1,0:T(8,128)(2,1)S(1)}, u32[]{:S(2)}, u32[]{:S(2)}) collective-permute-start(bf16[4,96,1024]{2,1,0:T(8,128)(2,1)S(1)} %get-tuple-element.37), channel_id=1, source_target_pairs={{0,2},{1,3},{2,0},{3,1},{4,6},{5,7},{6,4},{7,5},{8,10},{9,11},{10,... | collective-permute-start | bytes 2359304 | tf_op jit(solution)/shard_map/ppermute | solution.py:372
  249.1 17.0 %collective-permute-start.5 = (bf16[4,32,3072]{2,1,0:T(8,128)(2,1)S(1)}, bf16[4,32,3072]{2,1,0:T(8,128)(2,1)S(1)}, u32[]{:S(2)}, u32[]{:S(2)}) collective-permute-start(bf16[4,32,3072]{2,1,0:T(8,128)(2,1)S(1)} %collective-permute-done.4.refs_0_), channel_id=1, source_target_pairs={{0,1},{1,0},{2,3},{3,2},{4,5},{5,4},{6,7},{7,6},{8,9},{9,8},{10,11... | collective-permute-start | bytes 2359304 | tf_op jit(solution)/shard_map/ppermute | solution.py:385
  250.3 17.5 %collective-permute-start.1 = (bf16[4,32,3072]{2,1,0:T(8,128)(2,1)S(1)}, bf16[4,32,3072]{2,1,0:T(8,128)(2,1)S(1)}, u32[]{:S(2)}, u32[]{:S(2)}) collective-permute-start(bf16[4,32,3072]{2,1,0:T(8,128)(2,1)S(1)} %collective-permute-done.refs_1_), channel_id=1, source_target_pairs={{0,1},{1,0},{2,3},{3,2},{4,5},{5,4},{6,7},{7,6},{8,9},{9,8},{10,11... | collective-permute-start | bytes 2359304 | tf_op jit(solution)/shard_map/ppermute | solution.py:385
  251.1 16.8 %collective-permute-start.3 = (bf16[4,96,1024]{2,1,0:T(8,128)(2,1)S(1)}, bf16[4,96,1024]{2,1,0:T(8,128)(2,1)S(1)}, u32[]{:S(2)}, u32[]{:S(2)}) collective-permute-start(bf16[4,96,1024]{2,1,0:T(8,128)(2,1)S(1)} %collective-permute-done.2.refs_2_), channel_id=1, source_target_pairs={{0,1},{1,0},{2,3},{3,2},{4,5},{5,4},{6,7},{7,6},{8,9},{9,8},{10,11... | collective-permute-start | bytes 2359304 | tf_op jit(solution)/shard_map/ppermute | solution.py:385

commit v2 on v1

--- a/solution.py
+++ b/solution.py
@@ -37,6 +37,7 @@
 
 PLACE, THEN = ring()
 TURN = {0: (0, 1, 1, 0), 1: (1, 1, 1, 1), 2: (0, 0, 0, 0), 3: (1, 1, 1, 1)}
+CROSS = ((0, (0, 1, 2, 3)), (1, (0, 1, 2, 3)), (2, (0, 1, 2)), (2, (3,)))
 FIRST = {(0, 0): 4, (0, 1): 8, (0, 3): 4, (1, 0): 8, (2, 0): 4, (3, 0): 4}
 
 
@@ -44,6 +45,11 @@
     d1, d2, d3 = order
     kept = [d2 ^ d3, d2, d3, 0]
     return [d1 ^ r for r in kept] + kept
+
+
+def far(order):
+    _, d2, d3 = order
+    return (0, d3, d2, d2 ^ d3)
 
 
 def total(refs):
@@ -54,9 +60,10 @@
 
 
 def kernel(*refs):
-    g, w, m, v, out_w, out_m, out_v, later, mine = (refs[i : i + 3] for i in range(0, 27, 3))
-    (pair_send, pair_first, pair_recv, pair_kept, mine_sem, rs_send, rs_recv) = refs[27:34]
-    (state_sem, free, ag_send, agp_send) = refs[34:]
+    g, w, m, v, out_w, out_m, out_v = (refs[i : i + 3] for i in range(0, 21, 3))
+    later, hand, mine = refs[21 : 21 + len(CROSS)], refs[21 + len(CROSS) : 24 + len(CROSS)], refs[24 + len(CROSS) : 27 + len(CROSS)]
+    (pair_send, pair_first, pair_recv, pair_kept, mine_sem, rs_send, rs_recv) = refs[27 + len(CROSS) : 34 + len(CROSS)]
+    (state_sem, free, ag_send, agp_send) = refs[34 + len(CROSS) :]
 
     me = lax.axis_index("dp")
     core = lax.rem(me, 2)
@@ -72,14 +79,19 @@
     peers = (partner, at(X), at(Y), at(Z))
     rows_of = [one.shape[1] for one in m]
 
-    def rows(k, mask, which, half):
+    def rows(k, mask, which, half, piece=None):
         size = rows_of[k] // HALVES
         start = (chip(mask) * 2 + which) * rows_of[k] + half * size
+        if piece is not None:
+            size = size // 2
+            start = start + piece * size
         return pl.ds(pl.multiple_of(start, TILE), size)
 
-    def part(k, half, slot=0):
+    def part(k, half, slot=0, piece=None):
         size = rows_of[k] // HALVES
-        return pl.ds(slot * rows_of[k] + half * size, size)
+        if piece is None:
+            return pl.ds(slot * rows_of[k] + half * size, size)
+        return pl.ds(slot * rows_of[k] + half * size + piece * (size // 2), size // 2)
 
     def remote(src, dst, send, recv, device):
         return pltpu.make_async_remote_copy(
@@ -96,30 +108,34 @@
                 source = g[k].at[layer, rows(k, r, core, half)]
                 pltpu.make_async_copy(source, mine[k].at[PLACE[stage, c] + j], mine_sem.at[TURN[stage][c], k]).start()
 
-    def pair(k, c, layer, half, slot):
+    def pair(k, c, layer, half, slot, piece=None):
         r = slots(ORDERS[k])[slot]
-        arrived = pair_kept.at[k] if slot > 3 else pair_recv.at[k, c - 1] if c else pair_first.at[k, slot]
-        here = out_w[k].at[layer, part(k, half, THEIRS + slot)]
-        return remote(g[k].at[layer, rows(k, r, 1 - core, half)], here, pair_send.at[k], arrived, partner)
-
-    for k in range(3):
-        load_mine(k, None)
+        arrived = pair_kept.at[k] if slot > 3 else pair_recv.at[k, c - 1] if c else pair_first.at[k, 4 if piece == 0 else slot]
+        here = out_w[k].at[layer, part(k, half, THEIRS + slot, piece)]
+        return remote(g[k].at[layer, rows(k, r, 1 - core, half, piece)], here, pair_send.at[k], arrived, partner)
 
     barrier = pltpu.get_barrier_semaphore()
     for peer in peers:
         pl.semaphore_signal(barrier, inc=1, device_id=peer, device_id_type=pl.DeviceIdType.MESH)
+    for k in range(3):
+        load_mine(k, None)
     pl.semaphore_wait(barrier, 4)
 
     def pair_chunk(c, group):
         for slot in range(4 * group, 4 * group + 4):
-            for k in range(3):
-                pair(k, c, *CHUNKS[c], slot).start()
+            for piece in (0, 1) if c == slot == 0 else (None,):
+                for k in range(3):
+                    pair(k, c, *CHUNKS[c], slot, piece).start()
 
     pair_chunk(0, 0)
     pair_chunk(1, 0)
 
     def arrival(k, blocks, sem):
         spot = out_w[k].at[0, pl.ds(0, blocks * rows_of[k] // HALVES)]
+        return remote(spot, spot, pair_send.at[k], sem, partner)
+
+    def half_arrival(k, sem):
+        spot = out_w[k].at[0, pl.ds(0, rows_of[k] // HALVES // 2)]
         return remote(spot, spot, pair_send.at[k], sem, partner)
 
     def departure(k, blocks, sem):
@@ -137,9 +153,10 @@
     def slot_rows(k, half, slot, i):
         return pl.ds(pl.multiple_of(slot * rows_of[k] + half * (rows_of[k] // HALVES) + i * step_of(k), TILE), step_of(k))
 
-    def add(k, c, layer, half, stage, begin, count, extra):
+    def add(k, c, layer, half, stage, begin, count, extra, piece=None):
         first = STAGES[stage][0] + begin
         steps = rows_of[k] // HALVES // step_of(k)
+        low, high = (0, count * steps) if piece is None else (piece * steps // 2, (piece + 1) * steps // 2)
 
         def body(n, _):
             j, i = lax.div(n, steps), lax.rem(n, steps)
@@ -149,23 +166,26 @@
             out_w[k][layer, here] = total(terms).astype(jnp.bfloat16)
             return 0
 
-        lax.fori_loop(0, count * steps, body, 0)
-
-    def hop(stage, k, c, layer, half, begin, count):
+        lax.fori_loop(low, high, body, 0)
+
+    def hop(stage, k, c, layer, half, begin, count, piece=None):
         first = STAGES[stage][0]
         land = (LAND1, LAND2, LAND3)[stage]
         for j in range(begin, begin + count):
-            source = out_w[k].at[layer, part(k, half, THEIRS + first + j)]
-            target = out_w[k].at[layer, part(k, half, land + j)]
+            source = out_w[k].at[layer, part(k, half, THEIRS + first + j, piece)]
+            target = out_w[k].at[layer, part(k, half, land + j, piece)]
             remote(source, target, rs_send.at[k, c], rs_recv.at[stage, k, c], at(ORDERS[k][stage])).start()
 
-    for slot in range(4):
+    for slot, piece in ((0, 0), (0, 1), (1, None), (2, None), (3, None)):
         for k in range(3):
+            if piece == 0:
+                wait_mine(k, 0, 0)
             if slot == 0:
-                wait_mine(k, 0, 0)
-            arrival(k, 1, pair_first.at[k, slot]).wait_recv()
-            add(k, 0, *CHUNKS[0], 0, slot, 1, [])
-            hop(0, k, 0, *CHUNKS[0], slot, 1)
+                half_arrival(k, pair_first.at[k, 4 * (1 - piece)]).wait_recv()
+            else:
+                arrival(k, 1, pair_first.at[k, slot]).wait_recv()
+            add(k, 0, *CHUNKS[0], 0, slot, 1, [], piece)
+            hop(0, k, 0, *CHUNKS[0], slot, 1, piece)
     for c, group in ((2, 0), (3, 0), (0, 1), (1, 1), (2, 1), (3, 1)):
         pair_chunk(c, group)
     for k in range(3):
@@ -228,22 +248,23 @@
             return rs_recv.at[(d3, d2, d2 ^ d3).index(mask), k, c]
         return pair_first.at[k, (0, d3, d2, d2 ^ d3).index(mask ^ d1)] if c == LAST - 1 else pair_recv.at[k, c]
 
-    def set_aside(k, layer, half, mask, place):
+    def set_aside(k, layer, half, mask, target):
         start = (chip(mask) * 2 + core) * rows_of[k] + half * (rows_of[k] // HALVES)
 
         def body(i, _):
             there = pl.ds(pl.multiple_of(start + i * step_of(k), TILE), step_of(k))
-            later[k][place, slot_rows(k, 0, 0, i)] = out_w[k][layer, there]
+            target[slot_rows(k, 0, 0, i)] = out_w[k][layer, there]
             return 0
 
         lax.fori_loop(0, rows_of[k] // HALVES // step_of(k), body, 0)
 
     def gather(k, c, layer, half, mask, dim):
-        _, d2, d3 = ORDERS[k]
         d = ORDERS[k][dim]
         spot = out_w[k].at[layer, rows(k, mask, core, half)]
         if dim == 0 and c == LAST:
-            set_aside(k, layer, half, mask, (0, d3, d2, d2 ^ d3).index(mask))
+            place = far(ORDERS[k]).index(mask)
+            (target,) = [later[i].at[places.index(place)] for i, (which, places) in enumerate(CROSS) if which == k and place in places]
+            set_aside(k, layer, half, mask, target)
         else:
             remote(spot, spot, ag_send.at[k], gathered(k, c, mask ^ d), at(d)).start()
 
@@ -281,54 +302,76 @@
             gather(k, c, layer, half, d3, dim)
         to_partner(k, layer, half, d3).start()
     for c, (layer, half) in enumerate(CHUNKS):
-        for far in range(2):
+        for both in range(2):
             for k, (d1, d2, d3) in enumerate(ORDERS):
-                mask = d2 ^ d3 * far
+                mask = d2 ^ d3 * both
                 wait_gather(k, c, mask)
                 gather(k, c, layer, half, mask, 0)
                 to_partner(k, layer, half, mask).start()
     for c, (layer, half) in enumerate(CHUNKS[:LAST]):
         for which in range(4):
-            for k, (d1, d2, d3) in enumerate(ORDERS):
+            for k, order in enumerate(ORDERS):
+                mask = order[0] ^ far(order)[which]
                 if c == LAST - 1:
                     arrival(k, 1, pair_first.at[k, which]).wait_recv()
                 elif which == 0:
                     arrival(k, 4, pair_recv.at[k, c]).wait_recv()
-                to_partner(k, layer, half, d1 ^ (0, d3, d2, d2 ^ d3)[which]).start()
+                if c == LAST - 1 and which == 3:
+                    set_aside(k, layer, half, mask, hand[k])
+                else:
+                    to_partner(k, layer, half, mask).start()
 
     n = len(CHUNKS)
     for k in range(3):
         departure(k, 8 * n, pair_send.at[k]).wait_send()
         departure(k, 7 * n - 4, ag_send.at[k]).wait_send()
-        departure(k, 8 * n - 4, agp_send.at[k]).wait_send()
-        arrival(k, 8 * n - 4, pair_kept.at[k]).wait_recv()
+        departure(k, 8 * n - 5, agp_send.at[k]).wait_send()
+        arrival(k, 8 * n - 5, pair_kept.at[k]).wait_recv()
+
+
+def place_of(mask, size):
+    me = lax.axis_index("dp")
+    bits = {Z: lax.rem(lax.div(me, 2), 2), Y: lax.rem(lax.div(me, 4), 2), X: lax.div(me, 8)}
+    return sum(d * ((1 - bits[d]) if mask & d else bits[d]) for d in (X, Y, Z)) * 2 * size
 
 
 def put_out(*refs):
     sources, targets, sem = refs[:9], refs[9:18], refs[18]
-    for i, (source, target) in enumerate(zip(sources, targets, strict=True)):
-        for layer in range(LAYERS):
-            for j in range(4):
-                here = pl.ds(j * (source.shape[1] // 4), source.shape[1] // 4)
-                pltpu.make_async_copy(source.at[layer, here], target.at[layer, here], sem.at[i]).start()
-    for i, (source, target) in enumerate(zip(sources, targets, strict=True)):
-        pltpu.make_async_copy(source, target, sem.at[i]).wait()
+
+    def put(i, layer, start, size, which):
+        here = pl.ds(start, size)
+        pltpu.make_async_copy(sources[i].at[layer, here], targets[i].at[layer, here], sem.at[which]).start()
+
+    layer, half = CHUNKS[LAST]
+    for k, (d1, d2, d3) in enumerate(ORDERS):
+        size = sources[k].shape[1] // 16
+        for j in range(4):
+            put(k, 1 - layer, j * 4 * size, 4 * size, k)
+        for r in (0, d3, d2, d2 ^ d3):
+            put(k, layer, pl.multiple_of(place_of(r, size), TILE), 2 * size, 9 + k)
+            for core in range(2):
+                start = place_of(d1 ^ r, size) + core * size + (1 - half) * (size // HALVES)
+                put(k, layer, pl.multiple_of(start, TILE), size // HALVES, 9 + k)
+    for i in range(3, 9):
+        for j in range(LAYERS):
+            put(i, j, 0, sources[i].shape[1], i)
+    for k in range(3):
+        size = sources[k].shape[1] // 16
+        for which, there in ((k, sources[k].at[0]), (9 + k, sources[k].at[0, pl.ds(0, 12 * size)])):
+            pltpu.make_async_copy(there, there, sem.at[which]).wait()
+    for i in range(3, 9):
+        pltpu.make_async_copy(sources[i], sources[i], sem.at[i]).wait()
 
 
 def put_rest(items, *refs):
     n = len(items)
     sources, out_w, sem = refs[:n], refs[n + 3 : n + 6], refs[n + 6]
-    me = lax.axis_index("dp")
-    core = lax.rem(me, 2)
-    bits = {Z: lax.rem(lax.div(me, 2), 2), Y: lax.rem(lax.div(me, 4), 2), X: lax.div(me, 8)}
-    layer, half = CHUNKS[LAST]
-    for i, (k, whose) in enumerate(items):
-        d1, d2, d3 = ORDERS[k]
-        size = sources[i].shape[1]
-        for j, r in enumerate((0, d3, d2, d2 ^ d3)):
-            chip = sum(d * ((1 - bits[d]) if (d1 ^ r) & d else bits[d]) for d in (X, Y, Z))
-            which = 1 - core if whose else core
-            start = ((chip * 2 + which) * HALVES + half) * size
+    core = lax.rem(lax.axis_index("dp"), 2)
+    for i, (k, c, masks, whose) in enumerate(items):
+        layer, half = CHUNKS[c]
+        size = sources[i].shape[-2]
+        for j, mask in enumerate(masks):
+            start = place_of(mask, HALVES * size) + ((1 - core if whose else core) * HALVES + half) * size
             target = out_w[k].at[layer, pl.ds(pl.multiple_of(start, TILE), size)]
             pltpu.make_async_copy(sources[i].at[j], target, sem.at[i]).start()
     for i in range(n):
@@ -346,13 +389,14 @@
         out = pl.pallas_call(
             kernel,
             out_shape=[pltpu.VMEM(one.shape, one.dtype) for one in (*weights, *m, *v)]
-            + [pltpu.VMEM((4, rows // HALVES, columns), jnp.bfloat16) for rows, columns in blocks],
+            + [pltpu.VMEM((len(places), blocks[k][0] // HALVES, blocks[k][1]), jnp.bfloat16) for k, places in CROSS]
+            + [pltpu.VMEM((rows // HALVES, columns), jnp.bfloat16) for rows, columns in blocks],
             in_specs=[pl.BlockSpec(memory_space=pl.ANY)] * 12,
-            out_specs=[pl.BlockSpec(memory_space=pltpu.VMEM)] * 12,
+            out_specs=[pl.BlockSpec(memory_space=pltpu.VMEM)] * (12 + len(CROSS)),
             scratch_shapes=[
                 *[pltpu.VMEM((RING, rows // HALVES, columns), jnp.bfloat16) for rows, columns in blocks],
                 dma((3,)),
-                dma((3, 4)),
+                dma((3, 5)),
                 dma((3, n - 1)),
                 dma((3,)),
                 dma((2, 3)),
@@ -366,26 +410,36 @@
             compiler_params=pltpu.CompilerParams(collective_id=0, has_side_effects=True, vmem_limit_bytes=VMEM),
             name="step",
         )(*terms, *weights, *m, *v)
-        out, later = out[:9], out[9:]
+        out, later, hand = out[:9], out[9:-3], out[-3:]
+        swap = [(i, i ^ 1) for i in range(16)]
         own = []
+        for i, (k, _) in enumerate(CROSS):
+            own.append(lax.ppermute(later[i], "dp", [(i, i ^ 2 * ORDERS[k][0]) for i in range(16)]))
+        handed = []
         for k in range(3):
-            own.append(lax.ppermute(later[k], "dp", [(i, i ^ 2 * ORDERS[k][0]) for i in range(16)]))
+            handed.append(lax.ppermute(hand[k], "dp", swap)[None])
         out = pl.pallas_call(
             put_out,
             out_shape=[jax.ShapeDtypeStruct(one.shape, one.dtype) for one in (*weights, *m, *v)],
             in_specs=[pl.BlockSpec(memory_space=pl.ANY)] * 9,
             out_specs=[pl.BlockSpec(memory_space=pl.ANY)] * 9,
-            scratch_shapes=[dma((9,))],
+            scratch_shapes=[dma((12,))],
             cost_estimate=pl.CostEstimate(flops=30_000_000, bytes_accessed=48_000_000, transcendentals=0),
             compiler_params=pltpu.CompilerParams(vmem_limit_bytes=VMEM),
             name="put_out",
         )(*out)
         other = []
-        for k in range(3):
-            other.append(lax.ppermute(own[k], "dp", [(i, i ^ 1) for i in range(16)]))
-        arrived = {(k, whose): (own, other)[whose][k] for k in range(3) for whose in range(2)}
+        for i in range(len(CROSS)):
+            other.append(lax.ppermute(own[i], "dp", swap))
+        arrived = {}
+        for i, (k, places) in enumerate(CROSS):
+            masks = tuple(ORDERS[k][0] ^ far(ORDERS[k])[place] for place in places)
+            arrived[k, LAST, masks, 0], arrived[k, LAST, masks, 1] = own[i], other[i]
+        for k, order in enumerate(ORDERS):
+            arrived[k, LAST - 1, (order[0] ^ far(order)[3],), 1] = handed[k]
+        final = [item for item, block in arrived.items() if any(block is one for one in (other[0], other[1], other[3]))]
         new = out[:3]
-        for items in (((0, 0), (1, 0), (2, 0), (0, 1)), ((1, 1), (2, 1))):
+        for items in ([item for item in arrived if item not in final], final):
             n = len(items)
             new = pl.pallas_call(
                 functools.partial(put_rest, items),

time: 269 us -> 275 us (1.022)
  waiting for transfers between devices: 18 us -> 24.5 us
  Pallas kernels: 247 us -> 244 us
    ppermute x6 -> x11, waiting for transfers between devices: 18 us -> 24.5 us  [the longest x4 23.6 us: step(): lax.ppermute(later[i], 'dp', [(i, i ^ 2 * ORDERS[k][0]) for i in range(16)])]
  transfers between devices with their start and end apart: 6 -> 11, of which waited for: 3 -> 4; matrix products, arithmetic and copies ran while one was open for 0% -> 0% of each run, Pallas kernels for 6% -> 6%
where the time goes in v2:
time: 275 us
  Pallas kernels  244 us (89%)
  waiting for transfers between devices  24.5 us (9%)
  starting transfers between devices  5.18 us (2%)
    pallas_call x1, Pallas kernels, step(): pl.pallas_call(kernel, out_shape=[pltpu.VMEM(one.shape, one.dtype) for on...  228 us
    ppermute x4, waiting for transfers between devices, step(): lax.ppermute(later[i], 'dp', [(i, i ^ 2 * ORDERS[k][0]) for i in range(16)])  23.6 us
    pallas_call x1, Pallas kernels, step(): pl.pallas_call(put_out, out_shape=[jax.ShapeDtypeStruct(one.shape, one.dt...  13.6 us
  transfers between devices with their start and end apart: 11, of which 4 were waited for; matrix products, arithmetic and copies ran while one was open for 0% of the time, Pallas kernels for 6%

profile of v2, /device:TPU:0, one launch (start us, length us, event | category | flops | bytes accessed | tf_op | source)
XLA Modules:
  0.0 274.7 jit_solution(16390517748263360809)
XLA Ops:
  0.6 227.6 %step.1 = (bf16[2,1024,3072]{2,1,0:T(8,128)(2,1)S(1)}, bf16[2,1024,3072]{2,1,0:T(8,128)(2,1)S(1)}, bf16[2,3072,1024]{2,1,0:T(8,128)(2,1)S(1)}, f32[2,64,3072]{2,...) custom-call(bf16[2,1024,3072]{2,1,0:T(8,128)(2,1)} %bitcast.9, ...), custom_call_target="tpu_custom_call" | custom-call | tf_op jit(solution)/shard_map/step/pallas_call | solution.py:389
  228.2 1.5 collective-permute-start
  229.8 0.7 collective-permute-start.2
  230.5 1.3 collective-permute-start.6
  231.8 16.0 %collective-permute-done.refs_0_ = bf16[4,32,3072]{2,1,0:T(8,128)(2,1)S(1)} collective-permute-done((bf16[4,32,3072]{2,1,0:T(8,128)(2,1)S(1)}, bf16[4,32,3072]{2,1,0:T(8,128)(2,1)S(1)}, u32[]{:S(2)}, u32[]{:S(2)}) %collective-permute-start) | collective-permute-done | bytes 786464 | tf_op jit(solution)/shard_map/ppermute | solution.py:417
  247.8 0.0 collective-permute-start.1
  247.8 1.2 collective-permute-done.2.refs_1_
  249.0 0.0 collective-permute-start.3
  249.0 0.0 collective-permute-done.6.refs_2_
  249.0 0.5 collective-permute-start.7
  249.5 0.5 collective-permute-start.4
  250.0 0.0 collective-permute-start.8
  250.0 6.3 %collective-permute-done.4.refs_4_ = bf16[1,96,1024]{2,1,0:T(8,128)(2,1)S(1)} collective-permute-done((bf16[1,96,1024]{2,1,0:T(8,128)(2,1)S(1)}, bf16[1,96,1024]{2,1,0:T(8,128)(2,1)S(1)}, u32[]{:S(2)}, u32[]{:S(2)}) %collective-permute-start.4) | collective-permute-done | bytes 196640 | tf_op jit(solution)/shard_map/ppermute | solution.py:417
  256.3 0.0 collective-permute-start.9
  256.3 0.0 collective-permute-done.8
  256.3 0.5 collective-permute-start.10
  256.8 0.9 collective-permute-done.9
  257.8 0.1 collective-permute-start.5
  257.9 13.6 %put_out.1 = (bf16[2,1024,3072]{2,1,0:T(8,128)(2,1)}, bf16[2,1024,3072]{2,1,0:T(8,128)(2,1)}, bf16[2,3072,1024]{2,1,0:T(8,128)(2,1)}, f32[2,64,3072]{2,1,0:T(8,1...) custom-call(bf16[2,1024,3072]{2,1,0:T(8,128)(2,1)S(1)} %get-tuple-el, ...), custom_call_target="tpu_custom_call" | custom-call | flops 30000000 | bytes 48000000 | tf_op jit(solution)/shard_map/put_out/pallas_call | solution.py:421
  271.6 0.0 collective-permute-done.10
  271.6 0.0 collective-permute-done.7.refs_3_
  271.6 1.9 put_rest.2
  273.5 0.0 collective-permute-done.5.refs_2_
  273.5 0.0 collective-permute-done.1.refs_0_
  273.5 0.0 collective-permute-done.3.refs_1_
  273.5 1.2 put_rest.3
Async XLA Ops:
  228.2 19.6 %collective-permute-start = (bf16[4,32,3072]{2,1,0:T(8,128)(2,1)S(1)}, bf16[4,32,3072]{2,1,0:T(8,128)(2,1)S(1)}, u32[]{:S(2)}, u32[]{:S(2)}) collective-permute-start(bf16[4,32,3072]{2,1,0:T(8,128)(2,1)S(1)} %get-tuple-element.40), channel_id=1, source_target_pairs={{0,8},{1,9},{2,10},{3,11},{4,12},{5,13},{6,14},{7,15},{8,0},{9,1},... | collective-permute-start | bytes 2359304 | tf_op jit(solution)/shard_map/ppermute | solution.py:417
  229.8 19.2 %collective-permute-start.2 = (bf16[4,32,3072]{2,1,0:T(8,128)(2,1)S(1)}, bf16[4,32,3072]{2,1,0:T(8,128)(2,1)S(1)}, u32[]{:S(2)}, u32[]{:S(2)}) collective-permute-start(bf16[4,32,3072]{2,1,0:T(8,128)(2,1)S(1)} %get-tuple-element.41), channel_id=1, source_target_pairs={{0,4},{1,5},{2,6},{3,7},{4,0},{5,1},{6,2},{7,3},{8,12},{9,13},{10,... | collective-permute-start | bytes 2359304 | tf_op jit(solution)/shard_map/ppermute | solution.py:417
  230.5 18.5 %collective-permute-start.6 = (bf16[3,96,1024]{2,1,0:T(8,128)(2,1)S(1)}, bf16[3,96,1024]{2,1,0:T(8,128)(2,1)S(1)}, u32[]{:S(2)}, u32[]{:S(2)}) collective-permute-start(bf16[3,96,1024]{2,1,0:T(8,128)(2,1)S(1)} %get-tuple-element.43), channel_id=1, source_target_pairs={{0,2},{1,3},{2,0},{3,1},{4,6},{5,7},{6,4},{7,5},{8,10},{9,11},{10,... | collective-permute-start | bytes 1769480 | tf_op jit(solution)/shard_map/ppermute | solution.py:417
  247.8 25.7 %collective-permute-start.1 = (bf16[4,32,3072]{2,1,0:T(8,128)(2,1)S(1)}, bf16[4,32,3072]{2,1,0:T(8,128)(2,1)S(1)}, u32[]{:S(2)}, u32[]{:S(2)}) collective-permute-start(bf16[4,32,3072]{2,1,0:T(8,128)(2,1)S(1)} %collective-permute-done.refs_0_), channel_id=1, source_target_pairs={{0,1},{1,0},{2,3},{3,2},{4,5},{5,4},{6,7},{7,6},{8,9},{9,8},{10,11... | collective-permute-start | bytes 2359304 | tf_op jit(solution)/shard_map/ppermute | solution.py:433
  249.0 24.5 %collective-permute-start.3 = (bf16[4,32,3072]{2,1,0:T(8,128)(2,1)S(1)}, bf16[4,32,3072]{2,1,0:T(8,128)(2,1)S(1)}, u32[]{:S(2)}, u32[]{:S(2)}) collective-permute-start(bf16[4,32,3072]{2,1,0:T(8,128)(2,1)S(1)} %collective-permute-done.2.refs_1_), channel_id=1, source_target_pairs={{0,1},{1,0},{2,3},{3,2},{4,5},{5,4},{6,7},{7,6},{8,9},{9,8},{10,11... | collective-permute-start | bytes 2359304 | tf_op jit(solution)/shard_map/ppermute | solution.py:433
  249.0 22.6 %collective-permute-start.7 = (bf16[3,96,1024]{2,1,0:T(8,128)(2,1)S(1)}, bf16[3,96,1024]{2,1,0:T(8,128)(2,1)S(1)}, u32[]{:S(2)}, u32[]{:S(2)}) collective-permute-start(bf16[3,96,1024]{2,1,0:T(8,128)(2,1)S(1)} %collective-permute-done.6.refs_2_), channel_id=1, source_target_pairs={{0,1},{1,0},{2,3},{3,2},{4,5},{5,4},{6,7},{7,6},{8,9},{9,8},{10,11... | collective-permute-start | bytes 1769480 | tf_op jit(solution)/shard_map/ppermute | solution.py:433
  249.5 6.8 %collective-permute-start.4 = (bf16[1,96,1024]{2,1,0:T(8,128)(2,1)S(1)}, bf16[1,96,1024]{2,1,0:T(8,128)(2,1)S(1)}, u32[]{:S(2)}, u32[]{:S(2)}) collective-permute-start(bf16[1,96,1024]{2,1,0:T(8,128)(2,1)S(1)} %get-tuple-element.42), channel_id=1, source_target_pairs={{0,2},{1,3},{2,0},{3,1},{4,6},{5,7},{6,4},{7,5},{8,10},{9,11},{10,... | collective-permute-start | bytes 589832 | tf_op jit(solution)/shard_map/ppermute | solution.py:417
  250.0 6.3 %collective-permute-start.8 = (bf16[32,3072]{1,0:T(8,128)(2,1)S(1)}, bf16[32,3072]{1,0:T(8,128)(2,1)S(1)}, u32[]{:S(2)}, u32[]{:S(2)}) collective-permute-start(bf16[32,3072]{1,0:T(8,128)(2,1)S(1)} %get-tuple-element.44), channel_id=1, source_target_pairs={{0,1},{1,0},{2,3},{3,2},{4,5},{5,4},{6,7},{7,6},{8,9},{9,8},{10,11... | collective-permute-start | bytes 589832 | tf_op jit(solution)/shard_map/ppermute | solution.py:420
  256.3 1.4 collective-permute-start.9
  256.3 15.2 %collective-permute-start.10 = (bf16[96,1024]{1,0:T(8,128)(2,1)S(1)}, bf16[96,1024]{1,0:T(8,128)(2,1)S(1)}, u32[]{:S(2)}, u32[]{:S(2)}) collective-permute-start(bf16[96,1024]{1,0:T(8,128)(2,1)S(1)} %get-tuple-element.46), channel_id=1, source_target_pairs={{0,1},{1,0},{2,3},{3,2},{4,5},{5,4},{6,7},{7,6},{8,9},{9,8},{10,11... | collective-permute-start | bytes 589832 | tf_op jit(solution)/shard_map/ppermute | solution.py:420
  257.8 15.7 %collective-permute-start.5 = (bf16[1,96,1024]{2,1,0:T(8,128)(2,1)S(1)}, bf16[1,96,1024]{2,1,0:T(8,128)(2,1)S(1)}, u32[]{:S(2)}, u32[]{:S(2)}) collective-permute-start(bf16[1,96,1024]{2,1,0:T(8,128)(2,1)S(1)} %collective-permute-done.4.refs_4_), channel_id=1, source_target_pairs={{0,1},{1,0},{2,3},{3,2},{4,5},{5,4},{6,7},{7,6},{8,9},{9,8},{10,11... | collective-permute-start | bytes 589832 | tf_op jit(solution)/shard_map/ppermute | solution.py:433

commit v3 on v2

--- a/solution.py
+++ b/solution.py
@@ -110,7 +110,7 @@
 
     def pair(k, c, layer, half, slot, piece=None):
         r = slots(ORDERS[k])[slot]
-        arrived = pair_kept.at[k] if slot > 3 else pair_recv.at[k, c - 1] if c else pair_first.at[k, 4 if piece == 0 else slot]
+        arrived = pair_kept.at[k] if slot > 3 else pair_recv.at[k, c // 2] if c else pair_first.at[k, 4 if piece == 0 else slot]
         here = out_w[k].at[layer, part(k, half, THEIRS + slot, piece)]
         return remote(g[k].at[layer, rows(k, r, 1 - core, half, piece)], here, pair_send.at[k], arrived, partner)
 
@@ -174,7 +174,7 @@
         for j in range(begin, begin + count):
             source = out_w[k].at[layer, part(k, half, THEIRS + first + j, piece)]
             target = out_w[k].at[layer, part(k, half, land + j, piece)]
-            remote(source, target, rs_send.at[k, c], rs_recv.at[stage, k, c], at(ORDERS[k][stage])).start()
+            remote(source, target, rs_send.at[k, c // 2], rs_recv.at[stage, k, c // 2], at(ORDERS[k][stage])).start()
 
     for slot, piece in ((0, 0), (0, 1), (1, None), (2, None), (3, None)):
         for k in range(3):
@@ -192,7 +192,8 @@
         load_mine(k, (0, 0))
     for c, layer, half, k in events[3:]:
         wait_mine(k, c, 0)
-        arrival(k, 4, pair_recv.at[k, c - 1]).wait_recv()
+        if c < 3:
+            arrival(k, 4 * c, pair_recv.at[k, c // 2]).wait_recv()
         add(k, c, layer, half, 0, 0, 4, [])
         hop(0, k, c, layer, half, 0, 4)
         load_mine(k, (0, c))
@@ -213,13 +214,15 @@
         if c == 0:
             arrival(k, 4 * len(CHUNKS), pair_kept.at[k]).wait_recv()
         wait_mine(k, c, 1)
-        arrival(k, 4, rs_recv.at[0, k, c]).wait_recv()
+        if c % 2 == 0:
+            arrival(k, 8, rs_recv.at[0, k, c // 2]).wait_recv()
         add(k, c, layer, half, 1, 0, 2, [LAND1])
         hop(1, k, c, layer, half, 0, 2)
         load_mine(k, (1, c))
     for c, layer, half, k in events:
         wait_mine(k, c, 2)
-        arrival(k, 2, rs_recv.at[1, k, c]).wait_recv()
+        if c % 2 == 0:
+            arrival(k, 4, rs_recv.at[1, k, c // 2]).wait_recv()
         add(k, c, layer, half, 2, 0, 1, [LAND1 + 2, LAND2])
         hop(2, k, c, layer, half, 0, 1)
 
@@ -245,7 +248,7 @@
     def gathered(k, c, mask):
         d1, d2, d3 = ORDERS[k]
         if not mask & d1:
-            return rs_recv.at[(d3, d2, d2 ^ d3).index(mask), k, c]
+            return rs_recv.at[(d3, d2, d2 ^ d3).index(mask), k, c // 2]
         return pair_first.at[k, (0, d3, d2, d2 ^ d3).index(mask ^ d1)] if c == LAST - 1 else pair_recv.at[k, c]
 
     def set_aside(k, layer, half, mask, target):
@@ -269,31 +272,33 @@
             remote(spot, spot, ag_send.at[k], gathered(k, c, mask ^ d), at(d)).start()
 
     def wait_gather(k, c, mask):
-        arrival(k, 1, gathered(k, c, mask)).wait_recv()
+        if c % 2 == 0:
+            arrival(k, 2, gathered(k, c, mask)).wait_recv()
 
     def to_partner(k, layer, half, mask):
         spot = out_w[k].at[layer, rows(k, mask, core, half)]
         return remote(spot, spot, agp_send.at[k], pair_kept.at[k], partner)
 
-    def send_own(c, layer, half, k):
-        pl.semaphore_wait(free.at[k, c], 4)
-        for dim in (2, 1, 0):
-            gather(k, c, layer, half, 0, dim)
-        to_partner(k, layer, half, 0).start()
-
-    for n, (c, layer, half, k) in enumerate(events):
-        if c == 0:
-            held = out_w[k].at[0, pl.ds(0, 10 * rows_of[k])]
-            pltpu.make_async_copy(held, held, state_sem.at[k]).wait()
-        wait_mine(k, c, 3)
-        arrival(k, 1, rs_recv.at[2, k, c]).wait_recv()
-        departure(k, 7, rs_send.at[k, c]).wait_send()
-        adamw(k, c, layer, half)
-        for peer in peers:
-            pl.semaphore_signal(free.at[k, c], inc=1, device_id=peer, device_id_type=pl.DeviceIdType.MESH)
-        if n:
-            send_own(*events[n - 1])
-    send_own(*events[-1])
+    for first in range(0, len(CHUNKS), 2):
+        two = [event for event in events if event[0] // 2 == first // 2]
+        for c, layer, half, k in two:
+            if c == 0:
+                held = out_w[k].at[0, pl.ds(0, 10 * rows_of[k])]
+                pltpu.make_async_copy(held, held, state_sem.at[k]).wait()
+            wait_mine(k, c, 3)
+            if c == first:
+                arrival(k, 2, rs_recv.at[2, k, first // 2]).wait_recv()
+                departure(k, 14, rs_send.at[k, first // 2]).wait_send()
+            adamw(k, c, layer, half)
+            if c > first:
+                for peer in peers:
+                    pl.semaphore_signal(free.at[k, first // 2], inc=1, device_id=peer, device_id_type=pl.DeviceIdType.MESH)
+        for c, layer, half, k in two:
+            if c == first:
+                pl.semaphore_wait(free.at[k, first // 2], 4)
+            for dim in (2, 1, 0):
+                gather(k, c, layer, half, 0, dim)
+            to_partner(k, layer, half, 0).start()
 
     for c, layer, half, k in events:
         d1, d2, d3 = ORDERS[k]
@@ -397,13 +402,13 @@
                 *[pltpu.VMEM((RING, rows // HALVES, columns), jnp.bfloat16) for rows, columns in blocks],
                 dma((3,)),
                 dma((3, 5)),
-                dma((3, n - 1)),
+                dma((3, 2)),
                 dma((3,)),
                 dma((2, 3)),
-                dma((3, n)),
-                dma((3, 3, n)),
+                dma((3, n // 2)),
+                dma((3, 3, n // 2)),
                 dma((3,)),
-                pltpu.SemaphoreType.REGULAR((3, n)),
+                pltpu.SemaphoreType.REGULAR((3, n // 2)),
                 dma((3,)),
                 dma((3,)),
             ],
@@ -437,9 +442,10 @@
             arrived[k, LAST, masks, 0], arrived[k, LAST, masks, 1] = own[i], other[i]
         for k, order in enumerate(ORDERS):
             arrived[k, LAST - 1, (order[0] ^ far(order)[3],), 1] = handed[k]
-        final = [item for item, block in arrived.items() if any(block is one for one in (other[0], other[1], other[3]))]
+        calls = ((own[0], own[2], *handed), (own[1], own[3], other[0], other[2]), (other[1], other[3]))
+        rest = [[item for item, block in arrived.items() if any(block is one for one in call)] for call in calls]
         new = out[:3]
-        for items in ([item for item in arrived if item not in final], final):
+        for items in rest:
             n = len(items)
             new = pl.pallas_call(
                 functools.partial(put_rest, items),

time: 275 us -> 277 us (level)
  no operation moved by 1% of the time
where the time goes in v3:
time: 277 us
  Pallas kernels  245 us (88%)
  waiting for transfers between devices  25.8 us (9%)
  starting transfers between devices  5.35 us (2%)
    pallas_call x1, Pallas kernels, step(): pl.pallas_call(kernel, out_shape=[pltpu.VMEM(one.shape, one.dtype) for on...  227 us
    ppermute x4, waiting for transfers between devices, step(): lax.ppermute(later[i], 'dp', [(i, i ^ 2 * ORDERS[k][0]) for i in range(16)])  23.4 us
    pallas_call x1, Pallas kernels, step(): pl.pallas_call(put_out, out_shape=[jax.ShapeDtypeStruct(one.shape, one.dt...  13.6 us
  transfers between devices with their start and end apart: 11, of which 4 were waited for; matrix products, arithmetic and copies ran while one was open for 0% of the time, Pallas kernels for 6%

profile of v3, /device:TPU:0, one launch (start us, length us, event | category | flops | bytes accessed | tf_op | source)
XLA Modules:
  0.0 276.5 jit_solution(17749555412641930333)
XLA Ops:
  0.6 227.3 %step.1 = (bf16[2,1024,3072]{2,1,0:T(8,128)(2,1)S(1)}, bf16[2,1024,3072]{2,1,0:T(8,128)(2,1)S(1)}, bf16[2,3072,1024]{2,1,0:T(8,128)(2,1)S(1)}, f32[2,64,3072]{2,...) custom-call(bf16[2,1024,3072]{2,1,0:T(8,128)(2,1)} %bitcast.9, ...), custom_call_target="tpu_custom_call" | custom-call | tf_op jit(solution)/shard_map/step/pallas_call | solution.py:394
  227.9 1.5 collective-permute-start.4
  229.5 0.7 collective-permute-start
  230.2 1.3 collective-permute-start.6
  231.5 16.0 %collective-permute-done.4.refs_0_ = bf16[4,32,3072]{2,1,0:T(8,128)(2,1)S(1)} collective-permute-done((bf16[4,32,3072]{2,1,0:T(8,128)(2,1)S(1)}, bf16[4,32,3072]{2,1,0:T(8,128)(2,1)S(1)}, u32[]{:S(2)}, u32[]{:S(2)}) %collective-permute-start.4) | collective-permute-done | bytes 786464 | tf_op jit(solution)/shard_map/ppermute | solution.py:422
  247.5 0.0 collective-permute-start.5
  247.5 1.2 collective-permute-done.refs_1_
  248.7 0.0 collective-permute-start.1
  248.7 0.0 collective-permute-done.6.refs_1_
  248.7 0.5 collective-permute-start.7
  249.2 0.0 collective-permute-start.8
  249.2 0.5 collective-permute-start.9
  249.7 2.4 collective-permute-done.8
  252.1 0.8 collective-permute-start.2
  252.9 0.0 collective-permute-done.9
  252.9 0.0 collective-permute-start.10
  252.9 6.1 %collective-permute-done.2.refs_3_ = bf16[1,96,1024]{2,1,0:T(8,128)(2,1)S(1)} collective-permute-done((bf16[1,96,1024]{2,1,0:T(8,128)(2,1)S(1)}, bf16[1,96,1024]{2,1,0:T(8,128)(2,1)S(1)}, u32[]{:S(2)}, u32[]{:S(2)}) %collective-permute-start.2) | collective-permute-done | bytes 196640 | tf_op jit(solution)/shard_map/ppermute | solution.py:422
  259.1 0.0 collective-permute-start.3
  259.1 13.6 %put_out.1 = (bf16[2,1024,3072]{2,1,0:T(8,128)(2,1)}, bf16[2,1024,3072]{2,1,0:T(8,128)(2,1)}, bf16[2,3072,1024]{2,1,0:T(8,128)(2,1)}, f32[2,64,3072]{2,1,0:T(8,1...) custom-call(bf16[2,1024,3072]{2,1,0:T(8,128)(2,1)S(1)} %get-tuple-el, ...), custom_call_target="tpu_custom_call" | custom-call | flops 30000000 | bytes 48000000 | tf_op jit(solution)/shard_map/put_out/pallas_call | solution.py:426
  272.7 0.0 collective-permute-done.10
  272.7 1.3 put_rest.3
  274.1 0.0 collective-permute-done.7.refs_2_
  274.1 0.0 collective-permute-done.5.refs_0_
  274.1 1.4 put_rest.4
  275.5 0.0 collective-permute-done.3.refs_1_
  275.5 0.0 collective-permute-done.1.refs_0_
  275.6 1.0 put_rest.5
Async XLA Ops:
  227.9 19.6 %collective-permute-start.4 = (bf16[4,32,3072]{2,1,0:T(8,128)(2,1)S(1)}, bf16[4,32,3072]{2,1,0:T(8,128)(2,1)S(1)}, u32[]{:S(2)}, u32[]{:S(2)}) collective-permute-start(bf16[4,32,3072]{2,1,0:T(8,128)(2,1)S(1)} %get-tuple-element.45), channel_id=1, source_target_pairs={{0,8},{1,9},{2,10},{3,11},{4,12},{5,13},{6,14},{7,15},{8,0},{9,1},... | collective-permute-start | bytes 2359304 | tf_op jit(solution)/shard_map/ppermute | solution.py:422
  229.5 19.2 %collective-permute-start = (bf16[4,32,3072]{2,1,0:T(8,128)(2,1)S(1)}, bf16[4,32,3072]{2,1,0:T(8,128)(2,1)S(1)}, u32[]{:S(2)}, u32[]{:S(2)}) collective-permute-start(bf16[4,32,3072]{2,1,0:T(8,128)(2,1)S(1)} %get-tuple-element.43), channel_id=1, source_target_pairs={{0,4},{1,5},{2,6},{3,7},{4,0},{5,1},{6,2},{7,3},{8,12},{9,13},{10,... | collective-permute-start | bytes 2359304 | tf_op jit(solution)/shard_map/ppermute | solution.py:422
  230.2 18.5 %collective-permute-start.6 = (bf16[3,96,1024]{2,1,0:T(8,128)(2,1)S(1)}, bf16[3,96,1024]{2,1,0:T(8,128)(2,1)S(1)}, u32[]{:S(2)}, u32[]{:S(2)}) collective-permute-start(bf16[3,96,1024]{2,1,0:T(8,128)(2,1)S(1)} %get-tuple-element.46), channel_id=1, source_target_pairs={{0,2},{1,3},{2,0},{3,1},{4,6},{5,7},{6,4},{7,5},{8,10},{9,11},{10,... | collective-permute-start | bytes 1769480 | tf_op jit(solution)/shard_map/ppermute | solution.py:422
  247.5 26.6 %collective-permute-start.5 = (bf16[4,32,3072]{2,1,0:T(8,128)(2,1)S(1)}, bf16[4,32,3072]{2,1,0:T(8,128)(2,1)S(1)}, u32[]{:S(2)}, u32[]{:S(2)}) collective-permute-start(bf16[4,32,3072]{2,1,0:T(8,128)(2,1)S(1)} %collective-permute-done.4.refs_0_), channel_id=1, source_target_pairs={{0,1},{1,0},{2,3},{3,2},{4,5},{5,4},{6,7},{7,6},{8,9},{9,8},{10,11... | collective-permute-start | bytes 2359304 | tf_op jit(solution)/shard_map/ppermute | solution.py:438
  248.7 26.8 %collective-permute-start.1 = (bf16[4,32,3072]{2,1,0:T(8,128)(2,1)S(1)}, bf16[4,32,3072]{2,1,0:T(8,128)(2,1)S(1)}, u32[]{:S(2)}, u32[]{:S(2)}) collective-permute-start(bf16[4,32,3072]{2,1,0:T(8,128)(2,1)S(1)} %collective-permute-done.refs_1_), channel_id=1, source_target_pairs={{0,1},{1,0},{2,3},{3,2},{4,5},{5,4},{6,7},{7,6},{8,9},{9,8},{10,11... | collective-permute-start | bytes 2359304 | tf_op jit(solution)/shard_map/ppermute | solution.py:438
  248.7 25.3 %collective-permute-start.7 = (bf16[3,96,1024]{2,1,0:T(8,128)(2,1)S(1)}, bf16[3,96,1024]{2,1,0:T(8,128)(2,1)S(1)}, u32[]{:S(2)}, u32[]{:S(2)}) collective-permute-start(bf16[3,96,1024]{2,1,0:T(8,128)(2,1)S(1)} %collective-permute-done.6.refs_1_), channel_id=1, source_target_pairs={{0,1},{1,0},{2,3},{3,2},{4,5},{5,4},{6,7},{7,6},{8,9},{9,8},{10,11... | collective-permute-start | bytes 1769480 | tf_op jit(solution)/shard_map/ppermute | solution.py:438
  249.2 2.9 %collective-permute-start.8 = (bf16[32,3072]{1,0:T(8,128)(2,1)S(1)}, bf16[32,3072]{1,0:T(8,128)(2,1)S(1)}, u32[]{:S(2)}, u32[]{:S(2)}) collective-permute-start(bf16[32,3072]{1,0:T(8,128)(2,1)S(1)} %get-tuple-element.47), channel_id=1, source_target_pairs={{0,1},{1,0},{2,3},{3,2},{4,5},{5,4},{6,7},{7,6},{8,9},{9,8},{10,11... | collective-permute-start | bytes 589832 | tf_op jit(solution)/shard_map/ppermute | solution.py:425
  249.2 3.7 %collective-permute-start.9 = (bf16[32,3072]{1,0:T(8,128)(2,1)S(1)}, bf16[32,3072]{1,0:T(8,128)(2,1)S(1)}, u32[]{:S(2)}, u32[]{:S(2)}) collective-permute-start(bf16[32,3072]{1,0:T(8,128)(2,1)S(1)} %get-tuple-element.48), channel_id=1, source_target_pairs={{0,1},{1,0},{2,3},{3,2},{4,5},{5,4},{6,7},{7,6},{8,9},{9,8},{10,11... | collective-permute-start | bytes 589832 | tf_op jit(solution)/shard_map/ppermute | solution.py:425
  252.1 6.9 %collective-permute-start.2 = (bf16[1,96,1024]{2,1,0:T(8,128)(2,1)S(1)}, bf16[1,96,1024]{2,1,0:T(8,128)(2,1)S(1)}, u32[]{:S(2)}, u32[]{:S(2)}) collective-permute-start(bf16[1,96,1024]{2,1,0:T(8,128)(2,1)S(1)} %get-tuple-element.44), channel_id=1, source_target_pairs={{0,2},{1,3},{2,0},{3,1},{4,6},{5,7},{6,4},{7,5},{8,10},{9,11},{10,... | collective-permute-start | bytes 589832 | tf_op jit(solution)/shard_map/ppermute | solution.py:422
  252.9 19.8 %collective-permute-start.10 = (bf16[96,1024]{1,0:T(8,128)(2,1)S(1)}, bf16[96,1024]{1,0:T(8,128)(2,1)S(1)}, u32[]{:S(2)}, u32[]{:S(2)}) collective-permute-start(bf16[96,1024]{1,0:T(8,128)(2,1)S(1)} %get-tuple-element.49), channel_id=1, source_target_pairs={{0,1},{1,0},{2,3},{3,2},{4,5},{5,4},{6,7},{7,6},{8,9},{9,8},{10,11... | collective-permute-start | bytes 589832 | tf_op jit(solution)/shard_map/ppermute | solution.py:425
  259.1 16.5 %collective-permute-start.3 = (bf16[1,96,1024]{2,1,0:T(8,128)(2,1)S(1)}, bf16[1,96,1024]{2,1,0:T(8,128)(2,1)S(1)}, u32[]{:S(2)}, u32[]{:S(2)}) collective-permute-start(bf16[1,96,1024]{2,1,0:T(8,128)(2,1)S(1)} %collective-permute-done.2.refs_3_), channel_id=1, source_target_pairs={{0,1},{1,0},{2,3},{3,2},{4,5},{5,4},{6,7},{7,6},{8,9},{9,8},{10,11... | collective-permute-start | bytes 589832 | tf_op jit(solution)/shard_map/ppermute | solution.py:438

commit v4 on v3

--- a/solution.py
+++ b/solution.py
@@ -62,8 +62,8 @@
 def kernel(*refs):
     g, w, m, v, out_w, out_m, out_v = (refs[i : i + 3] for i in range(0, 21, 3))
     later, hand, mine = refs[21 : 21 + len(CROSS)], refs[21 + len(CROSS) : 24 + len(CROSS)], refs[24 + len(CROSS) : 27 + len(CROSS)]
-    (pair_send, pair_first, pair_recv, pair_kept, mine_sem, rs_send, rs_recv) = refs[27 + len(CROSS) : 34 + len(CROSS)]
-    (state_sem, free, ag_send, agp_send) = refs[34 + len(CROSS) :]
+    (pair_send, pair_first, pair_recv, pair_kept, mine_sem, rs_recv, free, agp_send) = refs[27 + len(CROSS) :]
+    state_sem = ag_send = pair_send
 
     me = lax.axis_index("dp")
     core = lax.rem(me, 2)
@@ -168,13 +168,16 @@
 
         lax.fori_loop(low, high, body, 0)
 
+    def rs_sent(k, c):
+        return pair_first.at[k, 0 if c // 2 else 4]
+
     def hop(stage, k, c, layer, half, begin, count, piece=None):
         first = STAGES[stage][0]
         land = (LAND1, LAND2, LAND3)[stage]
         for j in range(begin, begin + count):
             source = out_w[k].at[layer, part(k, half, THEIRS + first + j, piece)]
             target = out_w[k].at[layer, part(k, half, land + j, piece)]
-            remote(source, target, rs_send.at[k, c // 2], rs_recv.at[stage, k, c // 2], at(ORDERS[k][stage])).start()
+            remote(source, target, rs_sent(k, c), rs_recv.at[stage, k, c // 2], at(ORDERS[k][stage])).start()
 
     for slot, piece in ((0, 0), (0, 1), (1, None), (2, None), (3, None)):
         for k in range(3):
@@ -207,12 +210,12 @@
         ]
 
     for c, layer, half, k in events:
-        for copy in state(k, layer, half):
-            copy.start()
-
-    for c, layer, half, k in events:
         if c == 0:
             arrival(k, 4 * len(CHUNKS), pair_kept.at[k]).wait_recv()
+            departure(k, 8 * len(CHUNKS), pair_send.at[k]).wait_send()
+            for place in CHUNKS:
+                for copy in state(k, *place):
+                    copy.start()
         wait_mine(k, c, 1)
         if c % 2 == 0:
             arrival(k, 8, rs_recv.at[0, k, c // 2]).wait_recv()
@@ -288,7 +291,7 @@
             wait_mine(k, c, 3)
             if c == first:
                 arrival(k, 2, rs_recv.at[2, k, first // 2]).wait_recv()
-                departure(k, 14, rs_send.at[k, first // 2]).wait_send()
+                departure(k, 14, rs_sent(k, first)).wait_send()
             adamw(k, c, layer, half)
             if c > first:
                 for peer in peers:
@@ -328,7 +331,6 @@
 
     n = len(CHUNKS)
     for k in range(3):
-        departure(k, 8 * n, pair_send.at[k]).wait_send()
         departure(k, 7 * n - 4, ag_send.at[k]).wait_send()
         departure(k, 8 * n - 5, agp_send.at[k]).wait_send()
         arrival(k, 8 * n - 5, pair_kept.at[k]).wait_recv()
@@ -405,11 +407,8 @@
                 dma((3, 2)),
                 dma((3,)),
                 dma((2, 3)),
-                dma((3, n // 2)),
                 dma((3, 3, n // 2)),
-                dma((3,)),
                 pltpu.SemaphoreType.REGULAR((3, n // 2)),
-                dma((3,)),
                 dma((3,)),
             ],
             compiler_params=pltpu.CompilerParams(collective_id=0, has_side_effects=True, vmem_limit_bytes=VMEM),

time: 277 us -> 277 us (level)
  no operation moved by 1% of the time
where the time goes in v4:
time: 277 us; the launch traced here: 276 us
  Pallas kernels  245 us (88%)
  waiting for transfers between devices  25.8 us (9%)
  starting transfers between devices  5.35 us (2%)
    pallas_call x1, Pallas kernels, step(): pl.pallas_call(kernel, out_shape=[pltpu.VMEM(one.shape, one.dtype) for on...  227 us
    ppermute x4, waiting for transfers between devices, step(): lax.ppermute(later[i], 'dp', [(i, i ^ 2 * ORDERS[k][0]) for i in range(16)])  23.4 us
    pallas_call x1, Pallas kernels, step(): pl.pallas_call(put_out, out_shape=[jax.ShapeDtypeStruct(one.shape, one.dt...  13.6 us
  transfers between devices with their start and end apart: 11, of which 4 were waited for; matrix products, arithmetic and copies ran while one was open for 0% of the time, Pallas kernels for 6%

profile of v4, /device:TPU:0, one launch (start us, length us, event | category | flops | bytes accessed | tf_op | source)
XLA Modules:
  0.0 276.4 jit_solution(7118575469106566119)
XLA Ops:
  0.6 227.2 %step.1 = (bf16[2,1024,3072]{2,1,0:T(8,128)(2,1)S(1)}, bf16[2,1024,3072]{2,1,0:T(8,128)(2,1)S(1)}, bf16[2,3072,1024]{2,1,0:T(8,128)(2,1)S(1)}, f32[2,64,3072]{2,...) custom-call(bf16[2,1024,3072]{2,1,0:T(8,128)(2,1)} %bitcast.9, ...), custom_call_target="tpu_custom_call" | custom-call | tf_op jit(solution)/shard_map/step/pallas_call | solution.py:396
  227.8 1.5 collective-permute-start.4
  229.4 0.7 collective-permute-start
  230.1 1.3 collective-permute-start.6
  231.3 16.0 %collective-permute-done.4.refs_0_ = bf16[4,32,3072]{2,1,0:T(8,128)(2,1)S(1)} collective-permute-done((bf16[4,32,3072]{2,1,0:T(8,128)(2,1)S(1)}, bf16[4,32,3072]{2,1,0:T(8,128)(2,1)S(1)}, u32[]{:S(2)}, u32[]{:S(2)}) %collective-permute-start.4) | collective-permute-done | bytes 786464 | tf_op jit(solution)/shard_map/ppermute | solution.py:421
  247.4 0.0 collective-permute-start.5
  247.4 1.2 collective-permute-done.refs_1_
  248.6 0.0 collective-permute-start.1
  248.6 0.0 collective-permute-done.6.refs_1_
  248.6 0.5 collective-permute-start.7
  249.1 0.0 collective-permute-start.8
  249.1 0.5 collective-permute-start.9
  249.6 2.4 collective-permute-done.8
  252.0 0.8 collective-permute-start.2
  252.8 0.0 collective-permute-done.9
  252.8 0.0 collective-permute-start.10
  252.8 6.1 %collective-permute-done.2.refs_3_ = bf16[1,96,1024]{2,1,0:T(8,128)(2,1)S(1)} collective-permute-done((bf16[1,96,1024]{2,1,0:T(8,128)(2,1)S(1)}, bf16[1,96,1024]{2,1,0:T(8,128)(2,1)S(1)}, u32[]{:S(2)}, u32[]{:S(2)}) %collective-permute-start.2) | collective-permute-done | bytes 196640 | tf_op jit(solution)/shard_map/ppermute | solution.py:421
  259.0 0.0 collective-permute-start.3
  259.0 13.6 %put_out.1 = (bf16[2,1024,3072]{2,1,0:T(8,128)(2,1)}, bf16[2,1024,3072]{2,1,0:T(8,128)(2,1)}, bf16[2,3072,1024]{2,1,0:T(8,128)(2,1)}, f32[2,64,3072]{2,1,0:T(8,1...) custom-call(bf16[2,1024,3072]{2,1,0:T(8,128)(2,1)S(1)} %get-tuple-el, ...), custom_call_target="tpu_custom_call" | custom-call | flops 30000000 | bytes 48000000 | tf_op jit(solution)/shard_map/put_out/pallas_call | solution.py:425
  272.6 0.0 collective-permute-done.10
  272.6 1.3 put_rest.3
  274.0 0.0 collective-permute-done.7.refs_2_
  274.0 0.0 collective-permute-done.5.refs_0_
  274.0 1.4 put_rest.4
  275.4 0.0 collective-permute-done.3.refs_1_
  275.4 0.0 collective-permute-done.1.refs_0_
  275.4 1.0 put_rest.5
Async XLA Ops:
  227.8 19.6 %collective-permute-start.4 = (bf16[4,32,3072]{2,1,0:T(8,128)(2,1)S(1)}, bf16[4,32,3072]{2,1,0:T(8,128)(2,1)S(1)}, u32[]{:S(2)}, u32[]{:S(2)}) collective-permute-start(bf16[4,32,3072]{2,1,0:T(8,128)(2,1)S(1)} %get-tuple-element.45), channel_id=1, source_target_pairs={{0,8},{1,9},{2,10},{3,11},{4,12},{5,13},{6,14},{7,15},{8,0},{9,1},... | collective-permute-start | bytes 2359304 | tf_op jit(solution)/shard_map/ppermute | solution.py:421
  229.4 19.2 %collective-permute-start = (bf16[4,32,3072]{2,1,0:T(8,128)(2,1)S(1)}, bf16[4,32,3072]{2,1,0:T(8,128)(2,1)S(1)}, u32[]{:S(2)}, u32[]{:S(2)}) collective-permute-start(bf16[4,32,3072]{2,1,0:T(8,128)(2,1)S(1)} %get-tuple-element.43), channel_id=1, source_target_pairs={{0,4},{1,5},{2,6},{3,7},{4,0},{5,1},{6,2},{7,3},{8,12},{9,13},{10,... | collective-permute-start | bytes 2359304 | tf_op jit(solution)/shard_map/ppermute | solution.py:421
  230.1 18.5 %collective-permute-start.6 = (bf16[3,96,1024]{2,1,0:T(8,128)(2,1)S(1)}, bf16[3,96,1024]{2,1,0:T(8,128)(2,1)S(1)}, u32[]{:S(2)}, u32[]{:S(2)}) collective-permute-start(bf16[3,96,1024]{2,1,0:T(8,128)(2,1)S(1)} %get-tuple-element.46), channel_id=1, source_target_pairs={{0,2},{1,3},{2,0},{3,1},{4,6},{5,7},{6,4},{7,5},{8,10},{9,11},{10,... | collective-permute-start | bytes 1769480 | tf_op jit(solution)/shard_map/ppermute | solution.py:421
  247.4 26.6 %collective-permute-start.5 = (bf16[4,32,3072]{2,1,0:T(8,128)(2,1)S(1)}, bf16[4,32,3072]{2,1,0:T(8,128)(2,1)S(1)}, u32[]{:S(2)}, u32[]{:S(2)}) collective-permute-start(bf16[4,32,3072]{2,1,0:T(8,128)(2,1)S(1)} %collective-permute-done.4.refs_0_), channel_id=1, source_target_pairs={{0,1},{1,0},{2,3},{3,2},{4,5},{5,4},{6,7},{7,6},{8,9},{9,8},{10,11... | collective-permute-start | bytes 2359304 | tf_op jit(solution)/shard_map/ppermute | solution.py:437
  248.6 26.8 %collective-permute-start.1 = (bf16[4,32,3072]{2,1,0:T(8,128)(2,1)S(1)}, bf16[4,32,3072]{2,1,0:T(8,128)(2,1)S(1)}, u32[]{:S(2)}, u32[]{:S(2)}) collective-permute-start(bf16[4,32,3072]{2,1,0:T(8,128)(2,1)S(1)} %collective-permute-done.refs_1_), channel_id=1, source_target_pairs={{0,1},{1,0},{2,3},{3,2},{4,5},{5,4},{6,7},{7,6},{8,9},{9,8},{10,11... | collective-permute-start | bytes 2359304 | tf_op jit(solution)/shard_map/ppermute | solution.py:437
  248.6 25.3 %collective-permute-start.7 = (bf16[3,96,1024]{2,1,0:T(8,128)(2,1)S(1)}, bf16[3,96,1024]{2,1,0:T(8,128)(2,1)S(1)}, u32[]{:S(2)}, u32[]{:S(2)}) collective-permute-start(bf16[3,96,1024]{2,1,0:T(8,128)(2,1)S(1)} %collective-permute-done.6.refs_1_), channel_id=1, source_target_pairs={{0,1},{1,0},{2,3},{3,2},{4,5},{5,4},{6,7},{7,6},{8,9},{9,8},{10,11... | collective-permute-start | bytes 1769480 | tf_op jit(solution)/shard_map/ppermute | solution.py:437
  249.1 2.9 %collective-permute-start.8 = (bf16[32,3072]{1,0:T(8,128)(2,1)S(1)}, bf16[32,3072]{1,0:T(8,128)(2,1)S(1)}, u32[]{:S(2)}, u32[]{:S(2)}) collective-permute-start(bf16[32,3072]{1,0:T(8,128)(2,1)S(1)} %get-tuple-element.47), channel_id=1, source_target_pairs={{0,1},{1,0},{2,3},{3,2},{4,5},{5,4},{6,7},{7,6},{8,9},{9,8},{10,11... | collective-permute-start | bytes 589832 | tf_op jit(solution)/shard_map/ppermute | solution.py:424
  249.1 3.7 %collective-permute-start.9 = (bf16[32,3072]{1,0:T(8,128)(2,1)S(1)}, bf16[32,3072]{1,0:T(8,128)(2,1)S(1)}, u32[]{:S(2)}, u32[]{:S(2)}) collective-permute-start(bf16[32,3072]{1,0:T(8,128)(2,1)S(1)} %get-tuple-element.48), channel_id=1, source_target_pairs={{0,1},{1,0},{2,3},{3,2},{4,5},{5,4},{6,7},{7,6},{8,9},{9,8},{10,11... | collective-permute-start | bytes 589832 | tf_op jit(solution)/shard_map/ppermute | solution.py:424
  252.0 6.9 %collective-permute-start.2 = (bf16[1,96,1024]{2,1,0:T(8,128)(2,1)S(1)}, bf16[1,96,1024]{2,1,0:T(8,128)(2,1)S(1)}, u32[]{:S(2)}, u32[]{:S(2)}) collective-permute-start(bf16[1,96,1024]{2,1,0:T(8,128)(2,1)S(1)} %get-tuple-element.44), channel_id=1, source_target_pairs={{0,2},{1,3},{2,0},{3,1},{4,6},{5,7},{6,4},{7,5},{8,10},{9,11},{10,... | collective-permute-start | bytes 589832 | tf_op jit(solution)/shard_map/ppermute | solution.py:421
  252.8 19.8 %collective-permute-start.10 = (bf16[96,1024]{1,0:T(8,128)(2,1)S(1)}, bf16[96,1024]{1,0:T(8,128)(2,1)S(1)}, u32[]{:S(2)}, u32[]{:S(2)}) collective-permute-start(bf16[96,1024]{1,0:T(8,128)(2,1)S(1)} %get-tuple-element.49), channel_id=1, source_target_pairs={{0,1},{1,0},{2,3},{3,2},{4,5},{5,4},{6,7},{7,6},{8,9},{9,8},{10,11... | collective-permute-start | bytes 589832 | tf_op jit(solution)/shard_map/ppermute | solution.py:424
  259.0 16.5 %collective-permute-start.3 = (bf16[1,96,1024]{2,1,0:T(8,128)(2,1)S(1)}, bf16[1,96,1024]{2,1,0:T(8,128)(2,1)S(1)}, u32[]{:S(2)}, u32[]{:S(2)}) collective-permute-start(bf16[1,96,1024]{2,1,0:T(8,128)(2,1)S(1)} %collective-permute-done.2.refs_3_), channel_id=1, source_target_pairs={{0,1},{1,0},{2,3},{3,2},{4,5},{5,4},{6,7},{7,6},{8,9},{9,8},{10,11... | collective-permute-start | bytes 589832 | tf_op jit(solution)/shard_map/ppermute | solution.py:437

commit v5 on v4

--- a/solution.py
+++ b/solution.py
@@ -62,8 +62,9 @@
 def kernel(*refs):
     g, w, m, v, out_w, out_m, out_v = (refs[i : i + 3] for i in range(0, 21, 3))
     later, hand, mine = refs[21 : 21 + len(CROSS)], refs[21 + len(CROSS) : 24 + len(CROSS)], refs[24 + len(CROSS) : 27 + len(CROSS)]
-    (pair_send, pair_first, pair_recv, pair_kept, mine_sem, rs_recv, free, agp_send) = refs[27 + len(CROSS) :]
+    (pair_send, pair_first, pair_recv, pair_kept, mine_sem, rs_recv, free) = refs[27 + len(CROSS) :]
     state_sem = ag_send = pair_send
+    agp_send = mine_sem.at[0]
 
     me = lax.axis_index("dp")
     core = lax.rem(me, 2)
@@ -409,7 +410,6 @@
                 dma((2, 3)),
                 dma((3, 3, n // 2)),
                 pltpu.SemaphoreType.REGULAR((3, n // 2)),
-                dma((3,)),
             ],
             compiler_params=pltpu.CompilerParams(collective_id=0, has_side_effects=True, vmem_limit_bytes=VMEM),
             name="step",
@@ -441,7 +441,7 @@
             arrived[k, LAST, masks, 0], arrived[k, LAST, masks, 1] = own[i], other[i]
         for k, order in enumerate(ORDERS):
             arrived[k, LAST - 1, (order[0] ^ far(order)[3],), 1] = handed[k]
-        calls = ((own[0], own[2], *handed), (own[1], own[3], other[0], other[2]), (other[1], other[3]))
+        calls = ((own[0], own[2]), (own[1], own[3], other[2], *handed), (other[0], other[1], other[3]))
         rest = [[item for item, block in arrived.items() if any(block is one for one in call)] for call in calls]
         new = out[:3]
         for items in rest:

time: 277 us -> 275 us (level)
  no operation moved by 1% of the time
where the time goes in v5:
time: 275 us
  Pallas kernels  245 us (89%)
  waiting for transfers between devices  24.5 us (9%)
  starting transfers between devices  5.18 us (2%)
    pallas_call x1, Pallas kernels, step(): pl.pallas_call(kernel, out_shape=[pltpu.VMEM(one.shape, one.dtype) for on...  227 us
    ppermute x4, waiting for transfers between devices, step(): lax.ppermute(later[i], 'dp', [(i, i ^ 2 * ORDERS[k][0]) for i in range(16)])  23.6 us
    pallas_call x1, Pallas kernels, step(): pl.pallas_call(put_out, out_shape=[jax.ShapeDtypeStruct(one.shape, one.dt...  13.6 us
  transfers between devices with their start and end apart: 11, of which 4 were waited for; matrix products, arithmetic and copies ran while one was open for 0% of the time, Pallas kernels for 6%

profile of v5, /device:TPU:0, one launch (start us, length us, event | category | flops | bytes accessed | tf_op | source)
XLA Modules:
  0.0 274.9 jit_solution(7786474385152423113)
XLA Ops:
  0.6 227.2 %step.1 = (bf16[2,1024,3072]{2,1,0:T(8,128)(2,1)S(1)}, bf16[2,1024,3072]{2,1,0:T(8,128)(2,1)S(1)}, bf16[2,3072,1024]{2,1,0:T(8,128)(2,1)S(1)}, f32[2,64,3072]{2,...) custom-call(bf16[2,1024,3072]{2,1,0:T(8,128)(2,1)} %bitcast.9, ...), custom_call_target="tpu_custom_call" | custom-call | tf_op jit(solution)/shard_map/step/pallas_call | solution.py:397
  227.8 1.5 collective-permute-start
  229.3 0.7 collective-permute-start.2
  230.0 1.3 collective-permute-start.6
  231.3 16.0 %collective-permute-done.refs_0_ = bf16[4,32,3072]{2,1,0:T(8,128)(2,1)S(1)} collective-permute-done((bf16[4,32,3072]{2,1,0:T(8,128)(2,1)S(1)}, bf16[4,32,3072]{2,1,0:T(8,128)(2,1)S(1)}, u32[]{:S(2)}, u32[]{:S(2)}) %collective-permute-start) | collective-permute-done | bytes 786464 | tf_op jit(solution)/shard_map/ppermute | solution.py:421
  247.4 0.0 collective-permute-start.1
  247.4 1.2 collective-permute-done.2.refs_0_
  248.6 0.0 collective-permute-start.3
  248.6 0.0 collective-permute-done.6.refs_1_
  248.6 0.5 collective-permute-start.7
  249.1 0.5 collective-permute-start.4
  249.6 0.0 collective-permute-start.8
  249.6 6.3 %collective-permute-done.4.refs_2_ = bf16[1,96,1024]{2,1,0:T(8,128)(2,1)S(1)} collective-permute-done((bf16[1,96,1024]{2,1,0:T(8,128)(2,1)S(1)}, bf16[1,96,1024]{2,1,0:T(8,128)(2,1)S(1)}, u32[]{:S(2)}, u32[]{:S(2)}) %collective-permute-start.4) | collective-permute-done | bytes 196640 | tf_op jit(solution)/shard_map/ppermute | solution.py:421
  255.9 0.0 collective-permute-start.9
  255.9 0.0 collective-permute-done.8
  255.9 0.5 collective-permute-start.10
  256.4 0.9 collective-permute-done.9
  257.3 0.1 collective-permute-start.5
  257.5 13.6 %put_out.1 = (bf16[2,1024,3072]{2,1,0:T(8,128)(2,1)}, bf16[2,1024,3072]{2,1,0:T(8,128)(2,1)}, bf16[2,3072,1024]{2,1,0:T(8,128)(2,1)}, f32[2,64,3072]{2,1,0:T(8,1...) custom-call(bf16[2,1024,3072]{2,1,0:T(8,128)(2,1)S(1)} %get-tuple-el, ...), custom_call_target="tpu_custom_call" | custom-call | flops 30000000 | bytes 48000000 | tf_op jit(solution)/shard_map/put_out/pallas_call | solution.py:425
  271.1 1.1 put_rest.3
  272.2 0.0 collective-permute-done.10
  272.3 0.0 collective-permute-done.7.refs_1_
  272.3 1.4 put_rest.4
  273.7 0.0 collective-permute-done.5.refs_2_
  273.7 0.0 collective-permute-done.1.refs_0_
  273.7 0.0 collective-permute-done.3.refs_1_
  273.7 1.2 put_rest.5
Async XLA Ops:
  227.8 19.6 %collective-permute-start = (bf16[4,32,3072]{2,1,0:T(8,128)(2,1)S(1)}, bf16[4,32,3072]{2,1,0:T(8,128)(2,1)S(1)}, u32[]{:S(2)}, u32[]{:S(2)}) collective-permute-start(bf16[4,32,3072]{2,1,0:T(8,128)(2,1)S(1)} %get-tuple-element.43), channel_id=1, source_target_pairs={{0,8},{1,9},{2,10},{3,11},{4,12},{5,13},{6,14},{7,15},{8,0},{9,1},... | collective-permute-start | bytes 2359304 | tf_op jit(solution)/shard_map/ppermute | solution.py:421
  229.3 19.2 %collective-permute-start.2 = (bf16[4,32,3072]{2,1,0:T(8,128)(2,1)S(1)}, bf16[4,32,3072]{2,1,0:T(8,128)(2,1)S(1)}, u32[]{:S(2)}, u32[]{:S(2)}) collective-permute-start(bf16[4,32,3072]{2,1,0:T(8,128)(2,1)S(1)} %get-tuple-element.44), channel_id=1, source_target_pairs={{0,4},{1,5},{2,6},{3,7},{4,0},{5,1},{6,2},{7,3},{8,12},{9,13},{10,... | collective-permute-start | bytes 2359304 | tf_op jit(solution)/shard_map/ppermute | solution.py:421
  230.0 18.5 %collective-permute-start.6 = (bf16[3,96,1024]{2,1,0:T(8,128)(2,1)S(1)}, bf16[3,96,1024]{2,1,0:T(8,128)(2,1)S(1)}, u32[]{:S(2)}, u32[]{:S(2)}) collective-permute-start(bf16[3,96,1024]{2,1,0:T(8,128)(2,1)S(1)} %get-tuple-element.46), channel_id=1, source_target_pairs={{0,2},{1,3},{2,0},{3,1},{4,6},{5,7},{6,4},{7,5},{8,10},{9,11},{10,... | collective-permute-start | bytes 1769480 | tf_op jit(solution)/shard_map/ppermute | solution.py:421
  247.4 26.3 %collective-permute-start.1 = (bf16[4,32,3072]{2,1,0:T(8,128)(2,1)S(1)}, bf16[4,32,3072]{2,1,0:T(8,128)(2,1)S(1)}, u32[]{:S(2)}, u32[]{:S(2)}) collective-permute-start(bf16[4,32,3072]{2,1,0:T(8,128)(2,1)S(1)} %collective-permute-done.refs_0_), channel_id=1, source_target_pairs={{0,1},{1,0},{2,3},{3,2},{4,5},{5,4},{6,7},{7,6},{8,9},{9,8},{10,11... | collective-permute-start | bytes 2359304 | tf_op jit(solution)/shard_map/ppermute | solution.py:437
  248.6 25.1 %collective-permute-start.3 = (bf16[4,32,3072]{2,1,0:T(8,128)(2,1)S(1)}, bf16[4,32,3072]{2,1,0:T(8,128)(2,1)S(1)}, u32[]{:S(2)}, u32[]{:S(2)}) collective-permute-start(bf16[4,32,3072]{2,1,0:T(8,128)(2,1)S(1)} %collective-permute-done.2.refs_0_), channel_id=1, source_target_pairs={{0,1},{1,0},{2,3},{3,2},{4,5},{5,4},{6,7},{7,6},{8,9},{9,8},{10,11... | collective-permute-start | bytes 2359304 | tf_op jit(solution)/shard_map/ppermute | solution.py:437
  248.6 23.7 %collective-permute-start.7 = (bf16[3,96,1024]{2,1,0:T(8,128)(2,1)S(1)}, bf16[3,96,1024]{2,1,0:T(8,128)(2,1)S(1)}, u32[]{:S(2)}, u32[]{:S(2)}) collective-permute-start(bf16[3,96,1024]{2,1,0:T(8,128)(2,1)S(1)} %collective-permute-done.6.refs_1_), channel_id=1, source_target_pairs={{0,1},{1,0},{2,3},{3,2},{4,5},{5,4},{6,7},{7,6},{8,9},{9,8},{10,11... | collective-permute-start | bytes 1769480 | tf_op jit(solution)/shard_map/ppermute | solution.py:437
  249.1 6.8 %collective-permute-start.4 = (bf16[1,96,1024]{2,1,0:T(8,128)(2,1)S(1)}, bf16[1,96,1024]{2,1,0:T(8,128)(2,1)S(1)}, u32[]{:S(2)}, u32[]{:S(2)}) collective-permute-start(bf16[1,96,1024]{2,1,0:T(8,128)(2,1)S(1)} %get-tuple-element.45), channel_id=1, source_target_pairs={{0,2},{1,3},{2,0},{3,1},{4,6},{5,7},{6,4},{7,5},{8,10},{9,11},{10,... | collective-permute-start | bytes 589832 | tf_op jit(solution)/shard_map/ppermute | solution.py:421
  249.6 6.3 %collective-permute-start.8 = (bf16[32,3072]{1,0:T(8,128)(2,1)S(1)}, bf16[32,3072]{1,0:T(8,128)(2,1)S(1)}, u32[]{:S(2)}, u32[]{:S(2)}) collective-permute-start(bf16[32,3072]{1,0:T(8,128)(2,1)S(1)} %get-tuple-element.47), channel_id=1, source_target_pairs={{0,1},{1,0},{2,3},{3,2},{4,5},{5,4},{6,7},{7,6},{8,9},{9,8},{10,11... | collective-permute-start | bytes 589832 | tf_op jit(solution)/shard_map/ppermute | solution.py:424
  255.9 1.4 collective-permute-start.9
  255.9 16.3 %collective-permute-start.10 = (bf16[96,1024]{1,0:T(8,128)(2,1)S(1)}, bf16[96,1024]{1,0:T(8,128)(2,1)S(1)}, u32[]{:S(2)}, u32[]{:S(2)}) collective-permute-start(bf16[96,1024]{1,0:T(8,128)(2,1)S(1)} %get-tuple-element.49), channel_id=1, source_target_pairs={{0,1},{1,0},{2,3},{3,2},{4,5},{5,4},{6,7},{7,6},{8,9},{9,8},{10,11... | collective-permute-start | bytes 589832 | tf_op jit(solution)/shard_map/ppermute | solution.py:424
  257.3 16.3 %collective-permute-start.5 = (bf16[1,96,1024]{2,1,0:T(8,128)(2,1)S(1)}, bf16[1,96,1024]{2,1,0:T(8,128)(2,1)S(1)}, u32[]{:S(2)}, u32[]{:S(2)}) collective-permute-start(bf16[1,96,1024]{2,1,0:T(8,128)(2,1)S(1)} %collective-permute-done.4.refs_2_), channel_id=1, source_target_pairs={{0,1},{1,0},{2,3},{3,2},{4,5},{5,4},{6,7},{7,6},{8,9},{9,8},{10,11... | collective-permute-start | bytes 589832 | tf_op jit(solution)/shard_map/ppermute | solution.py:437
